TPU v7x, 32 devices: a whole 2x2x4 slice. The times are simulated.
32 devices in a mesh: rows: 8 (over z, x), grp: 4 (over y, core).
Axes of the slice: x: 2, y: 2, z: 4, core: 2. Of those that a mesh axis runs over, the one named last changes fastest.
Arguments:
- user_features: bfloat16 [4, 2048, 256], P('grp', 'rows'), may hold values from -72 to 72
- w_first: bfloat16 [256, 256], replicated, may hold values from -0.375 to 0.375
- w_second: bfloat16 [256, 256], replicated, may hold values from -0.375 to 0.375
- item_embed: bfloat16 [4, 2048, 256], P('grp', 'rows'), may hold values from -27 to 27
- example_weight: float32 [4, 2048], P('grp', 'rows'), may hold values from 0.02 to 0.2
- positive: int32 [4, 2048], P('grp', 'rows'), may hold values from 0 to 2047
- item_owner: int32 [4, 2048, 1], P('grp', 'rows'), may hold values from 0 to 7; in each aligned block of 256 rows (0 to 255, 256 to 511, ..., all dimensions but the last counted through in order) at most 128 rows name the same one
- item_row: int32 [4, 2048], P('grp', 'rows'), may hold values from 0 to 4095
Outputs:
- grad_first: float32 [256, 256], replicated
- grad_second: float32 [256, 256], replicated
- grad_table: float32 [32768, 256], P('rows', 'grp')
Inputs may be any that keep to these rules, and one draw needn't show every extreme that they name: `item_owner`: within the rows of one device (aligned blocks of 256 pairs of a group) no owner is named by more than 128 pairs, a bound that some block reaches.
All inputs are finite; a program needn't handle non-finite values.
Results may differ from a plain program's by a relative error of at most 0.0023.
The roundings to bfloat16 on the way count: a program that leaves them out, or rounds other values in their place, can miss the bound.
Values may be sent and summed in bfloat16 or wider, within the bound.
No kernel may reach another device: no remote copies, remote signals or barrier semaphores. Data moves between devices by JAX's collectives and lax.ppermute only.
A program may use at most 128 MiB of HBM per device.

v0:
```python
import jax
import jax.numpy as jnp
from jax import lax
from jax.sharding import PartitionSpec as P

ITEMS_DEV = 4096


def contract_first(left, right):
    return lax.dot_general(
        left, right, (((0,), (0,)), ((), ())), preferred_element_type=jnp.float32
    )


def contract_last(left, right):
    return lax.dot_general(
        left, right, (((1,), (1,)), ((), ())), preferred_element_type=jnp.float32
    )


def body(
    user_features, w_first, w_second, item_embed, example_weight, positive, item_owner, item_row
):
    features = user_features[0]
    own_items = item_embed[0]
    weights = example_weight[0]
    targets = positive[0]
    owners = item_owner[0, :, 0]
    item_rows = item_row[0]
    my_users = features.shape[0]
    feature_width = own_items.shape[1]
    peers = lax.axis_size("rows")
    my_index = lax.axis_index("rows")
    pre_act = jnp.dot(features, w_first, preferred_element_type=jnp.float32)
    hidden = jax.nn.silu(pre_act).astype(jnp.bfloat16)
    user_vecs = jnp.dot(hidden, w_second, preferred_element_type=jnp.float32).astype(jnp.bfloat16)
    gathered = lax.all_gather(own_items, "rows", axis=0, tiled=True)
    group_users = gathered.shape[0]
    scores = contract_last(user_vecs, gathered)
    row_max = jnp.max(scores, axis=1, keepdims=True)
    log_total = row_max + jnp.log(jnp.sum(jnp.exp(scores - row_max), axis=1, keepdims=True))
    columns = lax.broadcasted_iota(jnp.int32, (1, group_users), 1)
    chosen = (columns == targets[:, None]).astype(jnp.float32)
    dscore = (weights[:, None] * (jnp.exp(scores - log_total) - chosen)).astype(jnp.bfloat16)
    grad_user = jnp.dot(dscore, gathered, preferred_element_type=jnp.float32).astype(jnp.bfloat16)
    everyone = lax.all_gather(user_vecs, "rows", axis=0, tiled=True)
    target_all, total_all, weight_all = (
        lax.all_gather(targets.astype(jnp.float32), "rows", axis=0, tiled=True),
        lax.all_gather(log_total[:, 0], "rows", axis=0, tiled=True),
        lax.all_gather(weights, "rows", axis=0, tiled=True),
    )
    back_scores = contract_last(everyone, own_items)
    own_columns = my_index * my_users + lax.broadcasted_iota(jnp.int32, (1, my_users), 1)
    hits = (own_columns == target_all.astype(jnp.int32)[:, None]).astype(jnp.float32)
    back_dscore = (weight_all[:, None] * (jnp.exp(back_scores - total_all[:, None]) - hits)).astype(
        jnp.bfloat16
    )
    grad_item = contract_first(back_dscore, everyone)
    d_second = contract_first(hidden, grad_user)
    back_grad = contract_last(grad_user, w_second)
    sigmoid_pre = jax.nn.sigmoid(pre_act)
    grad_pre = (back_grad * sigmoid_pre * (1.0 + pre_act * (1.0 - sigmoid_pre))).astype(
        jnp.bfloat16
    )
    d_first = contract_first(features, grad_pre)
    grad_first, grad_second = lax.psum((d_first, d_second), ("rows", "grp"))
    capacity = max(2, 4 * my_users // peers)
    member = (owners[:, None] == lax.broadcasted_iota(jnp.int32, (1, peers), 1)).astype(jnp.int32)
    before = jnp.cumsum(member, axis=0) - member
    slot_rank = jnp.sum(before * member, axis=1)
    slots = owners * capacity + slot_rank
    send_grad = jnp.zeros((peers * capacity, feature_width), jnp.float32).at[slots].set(grad_item)
    send_grad = send_grad.reshape(peers, capacity, feature_width)
    send_rows = (
        jnp.full((peers * capacity,), -1.0, jnp.float32)
        .at[slots]
        .set(item_rows.astype(jnp.float32))
    )
    got_grad, got_rows = (
        lax.all_to_all(send_grad, "rows", split_axis=0, concat_axis=0, tiled=True),
        lax.all_to_all(
            send_rows.reshape(peers, capacity), "rows", split_axis=0, concat_axis=0, tiled=True
        ),
    )
    table_rows = got_rows.reshape(-1).astype(jnp.int32)
    table_rows = jnp.where(table_rows >= 0, table_rows, ITEMS_DEV)
    dense_grad = (
        jnp.zeros((ITEMS_DEV, feature_width), jnp.float32)
        .at[table_rows]
        .add(got_grad.reshape(-1, feature_width), mode="drop")
    )
    grad_table = lax.psum_scatter(dense_grad, "grp", scatter_dimension=1, tiled=True)
    return (grad_first, grad_second, grad_table)


def solution(mesh):
    placed = (
        P("grp", "rows", None),
        P(),
        P(),
        P("grp", "rows", None),
        P("grp", "rows"),
        P("grp", "rows"),
        P("grp", "rows", None),
        P("grp", "rows"),
    )
    return jax.shard_map(
        body, mesh=mesh, in_specs=placed, out_specs=(P(), P(), P("rows", "grp")), check_vma=False
    )
```

profile of v0, /device:TPU:0, one launch (start us, length us, event | category | flops | bytes accessed | tf_op | source)
XLA Modules:
  0.0 301.3 jit_solution(13880731240005856503)
XLA Ops:
  7.3 0.7 all-gather.9.cloned.1.call-update
  8.0 1.2 fusion.27
  9.2 0.9 convolution_convert_fusion
  10.1 0.7 convert_element_type.64
  11.7 2.0 scatter_custom_fusion
  13.7 7.3 %all-to-all-start = ((f32[8,1,128]{2,1,0:T(1,128)}), f32[8,1,128]{2,1,0:T(1,128)S(1)}, u32[]{:S(2)}, u32[]{:S(2)}) async-start(f32[8,1,128]{2,1,0:T(1,128)} %bitcast.13), calls=%async_computation | async-start | bytes 8192 | tf_op jit(solution)/shard_map/all_to_all | solution.py:81
  21.0 21.1 %all-gather.3 = f32[8,1,256]{2,1,0:T(1,128)S(1)} all-gather(f32[1,1,256]{2,1,0:T(1,128)S(1)} %bitcast.67), channel_id=1, replica_groups=mesh['rows'=8,'grp'=4] {'rows'}, dimensions={0}, use_global_device_ids=true | all-gather | bytes 9216 | tf_op jit(solution)/shard_map/all_gather | solution.py:48
  42.1 16.3 %all-gather.1 = f32[1,2048]{1,0:T(1,128)S(1)} all-gather(f32[1,256]{1,0:T(1,128)S(1)} %copy-done.4), channel_id=3, replica_groups=mesh['rows'=8,'grp'=4] {'rows'}, dimensions={1}, use_global_device_ids=true | all-gather | bytes 9216 | tf_op jit(solution)/shard_map/all_gather | solution.py:50
  58.4 1.9 fusion.37
  60.7 18.3 %all-gather.2 = f32[8,1,256]{2,1,0:T(1,128)S(1)} all-gather(f32[1,1,256]{2,1,0:T(1,128)S(1)} %bitcast.66), channel_id=1, replica_groups=mesh['rows'=8,'grp'=4] {'rows'}, dimensions={0}, use_global_device_ids=true | all-gather | bytes 9216 | tf_op jit(solution)/shard_map/all_gather | solution.py:49
  79.1 16.1 %all-gather.7.cloned.1.call-done = bf16[2048,256]{1,0:T(8,128)(2,1)} async-done(((bf16[256,256]{1,0:T(8,128)(2,1)}), bf16[2048,256]{1,0:T(8,128)(2,1)}) %all-gather.7.cloned.1.call-update) | async-done | bytes 1048592 | tf_op jit(solution)/shard_map/all_gather | solution.py:46
  95.2 3.9 %fusion.6 = f32[256,256]{1,0:T(8,128)} fusion(bf16[2048,256]{1,0:T(8,128)(2,1)} %all-gather.7.cloned.1.call-done, s32[256]{0:T(256)S(1)} %iota_add_fusion, f32[2048]{0:T(1024)S(1)} %bitcast.64, f32[2048]{0:T(1024)S(1)} %bitcast.63, s32[2048]{0:T(1024)S(1)} %bitcast.65, bf16[1,256,256]{2,1,0:T(8,128)(2,1)S(1)} %copy-done.2), kind=kOutput, calls=%fused_computation.13 | convolution fusion | flops 540016640 | bytes 1467392 | tf_op jit(solution)/shard_map/dot_general | solution.py:10
  99.1 2.9 scatter_custom_fusion.1
  102.0 4.4 %all-to-all-start.1 = ((f32[8,128,256]{2,1,0:T(8,128)}), f32[8,128,256]{2,1,0:T(8,128)}, u32[]{:S(2)}, u32[]{:S(2)}) async-start(f32[8,128,256]{2,1,0:T(8,128)} %bitcast.22), calls=%async_computation.1 | async-start | bytes 2097152 | tf_op jit(solution)/shard_map/all_to_all | solution.py:80
  106.4 0.8 convolution_convert_fusion.1
  107.8 1.0 fusion.36
  108.8 2.1 convolution_bitcast_fusion
  111.0 20.8 %all-to-all-done.1 = f32[8,128,256]{2,1,0:T(8,128)} async-done(((f32[8,128,256]{2,1,0:T(8,128)}), f32[8,128,256]{2,1,0:T(8,128)}, u32[]{:S(2)}, u32[]{:S(2)}) %all-to-all-start.1) | async-done | bytes 1048608 | tf_op jit(solution)/shard_map/all_to_all | solution.py:80
  131.8 8.7 %scatter_custom_fusion.2 = f32[4096,256]{1,0:T(8,128)} fusion(s32[1024]{0:T(1024)S(1)} %bitcast.68, f32[1024,256]{1,0:T(8,128)} %bitcast.23, f32[]{:T(128)} %constant.13.clone.1), kind=kCustom, calls=%fused_computation.8 | custom fusion | flops 262144 | bytes 4194816 | tf_op jit(solution)/shard_map/scatter-add | solution.py:90
  140.5 5.7 %copy.16 = f32[4096,256]{0,1:T(8,128)} copy(f32[4096,256]{1,0:T(8,128)} %scatter_custom_fusion.2) | data formatting | bytes 8388608
  146.2 100.4 %all-reduce.3.cloned.1.call-done = (f32[256,256]{0,1:T(8,128)}, f32[256,256]{1,0:T(8,128)}) async-done(((f32[256,256]{0,1:T(8,128)}, f32[256,256]{1,0:T(8,128)}), (f32[256,256]{0,1:T(8,128)}, f32[256,256]{1,0:T(8,128)})) %all-reduce.3.cloned.1.call-update) | async-done | bytes 524304 | tf_op jit(solution)/shard_map/psum | solution.py:66
  246.5 1.8 copy.14
  248.3 44.8 %reduce-scatter.4.cloned.1.call-done = f32[64,4096]{1,0:T(8,128)} async-done(((f32[256,4096]{1,0:T(8,128)}), f32[64,4096]{1,0:T(8,128)}) %reduce-scatter.4.cloned.1.call-update) | async-done | bytes 1048592
  293.1 1.7 copy.20
  (38 shorter events, 2.3 us)
Async XLA Ops:
  7.2 2.0 copy-start
  7.2 3.6 %copy-start.3 = (s32[1,256,1]{1,2,0:T(1,128)S(1)}, s32[1,256,1]{1,2,0:T(1,128)}, u32[]{:S(2)}) copy-start(s32[1,256,1]{1,2,0:T(1,128)} %param.14) | copy-start | bytes 3076
  7.2 13.8 %copy-start.5 = (s32[1,256]{1,0:T(1,128)S(1)}, s32[1,256]{1,0:T(1,128)}, u32[]{:S(2)}) copy-start(s32[1,256]{1,0:T(1,128)} %param.13) | copy-start | bytes 3076
  7.2 34.9 %copy-start.4 = (f32[1,256]{1,0:T(1,128)S(1)}, f32[1,256]{1,0:T(1,128)}, u32[]{:S(2)}) copy-start(f32[1,256]{1,0:T(1,128)} %param.12) | copy-start | bytes 3076
  7.2 51.2 %all-gather.9.cloned.1.call-start = ((), (), s32[]{:S(2)}) async-start(), calls=%async_computation.4 | async-start | bytes 1179648 | tf_op jit(solution)/shard_map/all_gather | solution.py:37
  7.9 87.2 %all-gather.7.cloned.1.call-start = ((), (), s32[]{:S(2)}) async-start(), calls=%async_computation.3 | async-start | bytes 1179648 | tf_op jit(solution)/shard_map/all_gather | solution.py:46
  13.7 88.3 %all-to-all-start = ((f32[8,1,128]{2,1,0:T(1,128)}), f32[8,1,128]{2,1,0:T(1,128)S(1)}, u32[]{:S(2)}, u32[]{:S(2)}) async-start(f32[8,1,128]{2,1,0:T(1,128)} %bitcast.13), calls=%async_computation | async-start | bytes 8192 | tf_op jit(solution)/shard_map/all_to_all | solution.py:81
  58.4 36.8 %copy-start.2 = (bf16[1,256,256]{2,1,0:T(8,128)(2,1)S(1)}, bf16[1,256,256]{2,1,0:T(8,128)(2,1)}, u32[]{:S(2)}) copy-start(bf16[1,256,256]{2,1,0:T(8,128)(2,1)} %param.11) | copy-start | bytes 393220
  99.1 7.3 %copy-start.1 = (bf16[1,2048,256]{2,1,0:T(8,128)(2,1)S(1)}, bf16[1,2048,256]{2,1,0:T(8,128)(2,1)}, u32[]{:S(2)}) copy-start(bf16[1,2048,256]{2,1,0:T(8,128)(2,1)} %all-gather.9.cloned.1.call-done) | copy-start | bytes 3145732
  102.0 4.4 %copy-start.6 = (s32[1,256]{1,0:T(1,128)S(1)}, s32[1,256]{1,0:T(1,128)}, u32[]{:S(2)}) copy-start(s32[1,256]{1,0:T(1,128)} %param.13) | copy-start | bytes 3076
  102.0 29.8 %all-to-all-start.1 = ((f32[8,128,256]{2,1,0:T(8,128)}), f32[8,128,256]{2,1,0:T(8,128)}, u32[]{:S(2)}, u32[]{:S(2)}) async-start(f32[8,128,256]{2,1,0:T(8,128)} %bitcast.22), calls=%async_computation.1 | async-start | bytes 2097152 | tf_op jit(solution)/shard_map/all_to_all | solution.py:80
  106.3 140.2 %all-reduce.3.cloned.1.call-start = ((), (), s32[]{:S(2)}) async-start(), calls=%async_computation.6 | async-start | bytes 1048576 | tf_op jit(solution)/shard_map/psum | solution.py:66
  107.2 0.6 copy-start.7
  111.0 182.1 %reduce-scatter.4.cloned.1.call-start = ((), (), s32[]{:S(2)}) async-start(), calls=%async_computation.5 | async-start | bytes 5242880
Sparse Core Ops, SparseCore 0:
  10.1 43.2 all-gather.8
  56.1 38.9 all-gather.6
  113.2 133.2 all-reduce.2
  249.5 43.5 reduce-scatter.3
where the time goes:
time: 302 us; the launch traced here: 301 us
  waiting for transfers between devices  183 us (61%)
  blocking collectives  55.7 us (18%)
  local copies, waits for them, and re-layouts  14.9 us (5%)
  between operations  13.9 us (5%)
  starting transfers between devices  11.8 us (4%)
  matrix products  11.7 us (4%)
  other arithmetic  10.6 us (4%)
    psum x1, waiting for transfers between devices, body(): grad_first, grad_second = lax.psum((d_first, d_second), ('rows', 'grp'))  100 us
    unnamed x5, waiting for transfers between devices  45.5 us
    all_gather x1, blocking collectives, body(): lax.all_gather(targets.astype(jnp.float32), 'rows', axis=0, tiled=True)  21.1 us
    all_to_all x1, waiting for transfers between devices, body(): lax.all_to_all(send_grad, 'rows', split_axis=0, concat_axis=0, tiled=True)  20.8 us
    all_gather x1, blocking collectives, body(): lax.all_gather(log_total[:, 0], 'rows', axis=0, tiled=True)  18.3 us
    all_gather x1, blocking collectives, body(): lax.all_gather(weights, 'rows', axis=0, tiled=True)  16.3 us
    all_gather x1, waiting for transfers between devices, body(): everyone = lax.all_gather(user_vecs, 'rows', axis=0, tiled=True)  16.1 us
    unnamed x19, local copies, waits for them, and re-layouts  9.79 us
  transfers between devices with their start and end apart: 6, of which 4 were waited for; matrix products, arithmetic and copies ran while one was open for 12% of the time, Pallas kernels for 0%

commit v1 on v0

--- a/solution.py
+++ b/solution.py
@@ -1,24 +1,396 @@
+import functools
+
 import jax
 import jax.numpy as jnp
 from jax import lax
+from jax.experimental import pallas as pl
+from jax.experimental.pallas import tpu as pltpu
 from jax.sharding import PartitionSpec as P
 
+
 ITEMS_DEV = 4096
+META = 16
+VMEM_BUDGET = 24 * 2**20
+BF16 = jnp.bfloat16
+F32 = jnp.float32
+
+
+def dot_nn(left, right):
+    return jnp.dot(left, right, preferred_element_type=F32)
 
 
 def contract_first(left, right):
-    return lax.dot_general(
-        left, right, (((0,), (0,)), ((), ())), preferred_element_type=jnp.float32
-    )
+    return lax.dot_general(left, right, (((0,), (0,)), ((), ())), preferred_element_type=F32)
 
 
 def contract_last(left, right):
-    return lax.dot_general(
-        left, right, (((1,), (1,)), ((), ())), preferred_element_type=jnp.float32
-    )
-
-
-def body(
+    return lax.dot_general(left, right, (((1,), (1,)), ((), ())), preferred_element_type=F32)
+
+
+def stack_rows(rows, width):
+    line = lax.broadcasted_iota(jnp.int32, (META, width), 0)
+    block = jnp.zeros((META, width), F32)
+    for at, row in enumerate(rows):
+        block = jnp.where(line == at, row, block)
+    return block.astype(BF16)
+
+
+def pack_kernel(
+    weight_hbm, target_hbm, owner_hbm, row_hbm, meta_ref, weight_ref, target_ref, owner_ref, row_ref, sems
+):
+    moves = [
+        (weight_hbm, weight_ref),
+        (target_hbm, target_ref),
+        (owner_hbm, owner_ref),
+        (row_hbm, row_ref),
+    ]
+    copies = [pltpu.make_async_copy(*move, sems.at[at]) for at, move in enumerate(moves)]
+    for copy in copies:
+        copy.start()
+    for copy in copies:
+        copy.wait()
+    weight = weight_ref[...]
+    high = weight.astype(BF16).astype(F32)
+    middle = (weight - high).astype(BF16).astype(F32)
+    low = weight - high - middle
+    rows = [owner_ref[...].astype(F32)]
+    for digits in (row_ref[...], target_ref[...]):
+        rows += [(digits >> 8).astype(F32), (digits & 255).astype(F32)]
+    meta_ref[...] = stack_rows([*rows, high, middle, low], weight.shape[1])
+
+
+def group_kernel(users, slots, begin, first, *refs):
+    user_refs, refs = refs[:users], refs[users:]
+    if first:
+        item_refs, refs = refs[:slots], refs[slots:]
+    else:
+        items_ref, refs = refs[0], refs[1:]
+    first_ref, second_ref = refs[:2]
+    refs = refs[2:]
+    if not first:
+        mine_in, other_in = refs[2:4]
+        refs = refs[4:]
+    dscore_ref, vecs_ref, mine_ref, other_ref = refs[:4]
+    refs = refs[4:]
+    if first:
+        items_ref, refs = refs[0], refs[1:]
+    scores_refs = refs
+    count = user_refs[0].shape[0] - META
+    lanes = 128
+    tall = 16
+    me = lax.axis_index("rows")
+    flip = lax.axis_index("grp") % 2 == 1
+    if first:
+        for slot in range(slots):
+            items_ref[slot * count : (slot + 1) * count, :] = item_refs[slot][...]
+    w_first = first_ref[...]
+    w_second = second_ref[...]
+    lane = lax.broadcasted_iota(jnp.int32, (tall, lanes), 1)
+
+    def span(slot):
+        return slice(slot * count, (slot + 1) * count)
+
+    state = []
+    for user in range(users):
+        features = user_refs[user][0:count, :]
+        meta = jnp.transpose(user_refs[user][count : count + META, :].astype(F32))
+        weight = meta[:, 5:6] + meta[:, 6:7] + meta[:, 7:8]
+        target = (meta[:, 3:4] * 256.0 + meta[:, 4:5]).astype(jnp.int32)
+        pre_act = dot_nn(features, w_first)
+        gate = jax.nn.sigmoid(pre_act)
+        hidden = (pre_act * gate).astype(BF16)
+        vecs = dot_nn(hidden, w_second).astype(BF16)
+        vecs_ref[:, span(begin + user)] = jnp.transpose(vecs)
+        state.append((weight, target, hidden, vecs))
+
+    def score(user, slot):
+        scores_refs[user][:, span(slot)] = contract_last(state[user][3], items_ref[span(slot), :])
+
+    def soften(user, line):
+        rows = slice(line * tall, (line + 1) * tall)
+        weight = state[user][0][rows]
+        away = lane - state[user][1][rows]
+        total_lanes = slots * count
+        parts = [scores_refs[user][rows, at : at + lanes] for at in range(0, total_lanes, lanes)]
+        top = parts[0]
+        for part in parts[1:]:
+            top = jnp.maximum(top, part)
+        top = jnp.max(top, axis=1, keepdims=True)
+        parts = [jnp.exp(part - top) for part in parts]
+        total = parts[0]
+        for part in parts[1:]:
+            total = total + part
+        scale = weight / jnp.sum(total, axis=1, keepdims=True)
+        for at, part in enumerate(parts):
+            start = at * lanes
+            base = (me ^ (start // count)) * count + start % count
+            part = part * scale
+            part = jnp.where(away == -base, part - weight, part)
+            out = slice((begin + user) * count + line * tall, (begin + user) * count + (line + 1) * tall)
+            dscore_ref[out, start : start + lanes] = part.astype(BF16)
+
+    def pull(user):
+        hidden = state[user][2]
+        half = slots * count // 2
+        grad_user = dot_nn(dscore_ref[span(begin + user), :half], items_ref[:half, :])
+        grad_user += dot_nn(dscore_ref[span(begin + user), half:], items_ref[half:, :])
+        grad_user = grad_user.astype(BF16)
+        d_second = contract_first(hidden, grad_user)
+        back = contract_last(grad_user, w_second)
+        features = user_refs[user][0:count, :]
+        pre_act = dot_nn(features, w_first)
+        gate = jax.nn.sigmoid(pre_act)
+        grad_pre = back * gate * (1.0 + pre_act * (1.0 - gate))
+        d_first = contract_first(features, grad_pre.astype(BF16))
+        return d_first, d_second
+
+    lines = count // tall
+    for slot in range(slots):
+        score(0, slot)
+    for user in range(users):
+        for line in range(lines):
+            soften(user, line)
+            if user + 1 < users and line % (lines // slots) == 0:
+                score(user + 1, line // (lines // slots))
+    for user in range(users):
+        d_first, d_second = pull(user)
+        mine = jnp.where(flip, d_second, d_first)
+        other = jnp.where(flip, d_first, d_second)
+        if user:
+            mine_ref[...] += mine
+            other_ref[...] += other
+        else:
+            mine_ref[...] = mine if first else mine_in[...] + mine
+            other_ref[...] = other if first else other_in[...] + other
+
+
+def select_slots(meta_refs, cap):
+    me = lax.axis_index("rows").astype(F32)
+    count = meta_refs[0].shape[1]
+    before = (
+        lax.broadcasted_iota(jnp.int32, (count, count), 0)
+        < lax.broadcasted_iota(jnp.int32, (count, count), 1)
+    ).astype(F32).astype(BF16)
+    place = lax.broadcasted_iota(jnp.int32, (cap, count), 0)
+    picks = []
+    for ref in meta_refs:
+        meta = ref[...].astype(F32)
+        owned = (meta == me).astype(F32)
+        rank = dot_nn(owned.astype(BF16), before)[0:1].astype(jnp.int32)
+        rank = jnp.where(owned[0:1] > 0.5, rank, -1)
+        picks.append((place == rank).astype(F32).astype(BF16))
+    return picks
+
+
+def rows_kernel(cap, slots, *refs):
+    metas, rows_ref = refs[:slots], refs[slots]
+    picks = select_slots(metas, cap)
+    for slot in range(slots):
+        digits = contract_last(metas[slot][...], picks[slot])
+        ones = contract_last(jnp.ones((META, picks[slot].shape[1]), BF16), picks[slot])
+        row = digits[1:2] * 256.0 + digits[2:3]
+        row = jnp.where(ones[0:1] > 0.5, row, -1.0)
+        rows_ref[:, slot * cap : (slot + 1) * cap] = jnp.broadcast_to(row, (8, cap))
+
+
+def compact_kernel(cap, slots, groups, steps, *refs):
+    dscore_ref, vecs_ref, refs = refs[0], refs[1], refs[2:]
+    metas, outs = refs[:slots], refs[slots:]
+    picks = select_slots(metas, cap)
+    count = metas[0].shape[1]
+    width = vecs_ref.shape[0] // groups
+    me = lax.axis_index("grp")
+    blocks = [partner(me, step, groups) for step in steps]
+    vecs = [vecs_ref[pl.ds(pl.multiple_of(one * width, width), width), :] for one in blocks]
+    vecs = jnp.concatenate(vecs, axis=0)
+    wide = min(2, slots)
+    for slot in range(0, slots, wide):
+        part = dot_nn(vecs, dscore_ref[:, slot * count : (slot + wide) * count]).astype(BF16)
+        for one in range(wide):
+            place = slice((slot + one) * cap, (slot + one + 1) * cap)
+            packed = contract_last(part[:, one * count : (one + 1) * count], picks[slot + one])
+            for at in range(len(steps)):
+                outs[at][:, place] = packed[at * width : (at + 1) * width].astype(BF16)
+
+
+def scatter_kernel(sources, first, *refs):
+    grads, rows, out_ref = refs[:sources], refs[sources : 2 * sources], refs[-1]
+    width, span = grads[0].shape
+    low_size = 256
+    high_size = out_ref.shape[1] // low_size
+    line = lax.broadcasted_iota(jnp.int32, (low_size, span), 0).astype(F32)
+    for source in range(sources):
+        row = rows[source][0:1, :]
+        high = jnp.floor(row / low_size)
+        low = row - high * low_size
+        onehot = (line == low).astype(F32).astype(BF16)
+        grad = grads[source][...].astype(F32)
+        left = jnp.concatenate(
+            [jnp.where(high == part, grad, 0.0).astype(BF16) for part in range(high_size)], axis=0
+        )
+        result = contract_last(left, onehot)
+        for part in range(high_size):
+            spot = slice(part * low_size, (part + 1) * low_size)
+            value = result[part * width : (part + 1) * width]
+            if source:
+                out_ref[:, spot] += value
+            else:
+                out_ref[:, spot] = value if first else refs[2 * sources][:, spot] + value
+
+
+VMEM = pl.BlockSpec(memory_space=pltpu.VMEM)
+
+
+def call(kernel, args, shapes, scratch=(), aliases=None, flops=1 << 20, limit=12):
+    return pl.pallas_call(
+        kernel,
+        out_shape=shapes,
+        in_specs=[VMEM] * len(args),
+        out_specs=[VMEM] * len(shapes),
+        scratch_shapes=list(scratch),
+        input_output_aliases=aliases or {},
+        compiler_params=pltpu.CompilerParams(vmem_limit_bytes=limit * 2**20),
+        cost_estimate=pl.CostEstimate(flops=flops, bytes_accessed=1 << 20, transcendentals=0),
+    )(*args)
+
+
+def partner(me, step, groups):
+    return me ^ step if groups & (groups - 1) == 0 else (me + step) % groups
+
+
+def to_partner(value, step, groups):
+    if step == 0:
+        return value
+    if groups & (groups - 1) == 0:
+        pairs = [(one, one ^ step) for one in range(groups)]
+    else:
+        pairs = [(one, (one + step) % groups) for one in range(groups)]
+    return lax.ppermute(value, "grp", pairs)
+
+
+def along(value, bit, size):
+    return lax.ppermute(value, "rows", [(one, one ^ bit) for one in range(size)])
+
+
+def gather_slots(own, size, early=()):
+    slots = [own]
+    for slot in range(1, size):
+        bit = slot & -slot
+        if slot in early:
+            bit = 1 << (slot.bit_length() - 1)
+        slots.append(along(slots[slot ^ bit], bit, size))
+    return slots
+
+
+def sum_towers(mine, other, groups):
+    if groups != 4:
+        mine, other = lax.psum((mine, other), "grp")
+        return mine, other
+    flip = lax.axis_index("grp") % 2 == 1
+    got = to_partner(other, 1, groups)
+    half = mine + got
+    got = to_partner(half, 2, groups)
+    half = half + got
+    rest = to_partner(half, 1, groups)
+    return jnp.where(flip, rest, half), jnp.where(flip, half, rest)
+
+
+def whole_group_body(*args):
+    return whole_group_step(*args)
+
+
+def whole_group_step(
+    user_features, w_first, w_second, item_embed, example_weight, positive, item_owner, item_row
+):
+    peers, groups = lax.axis_size("rows"), lax.axis_size("grp")
+    features, own_items = user_features[0], item_embed[0]
+    count, width = own_items.shape
+    cap = max(2, 4 * count // peers)
+    batch = min(2, peers)
+    args = [example_weight, positive, item_owner[:, :, 0], item_row]
+    line = (1, count)
+    meta = pl.pallas_call(
+        pack_kernel,
+        out_shape=jax.ShapeDtypeStruct((META, width), BF16),
+        in_specs=[pl.BlockSpec(memory_space=pltpu.HBM)] * len(args),
+        out_specs=VMEM,
+        scratch_shapes=[
+            pltpu.VMEM(line, F32),
+            pltpu.VMEM(line, jnp.int32),
+            pltpu.VMEM(line, jnp.int32),
+            pltpu.VMEM(line, jnp.int32),
+            pltpu.SemaphoreType.DMA((len(args),)),
+        ],
+        cost_estimate=pl.CostEstimate(flops=1 << 33, bytes_accessed=1 << 20, transcendentals=0),
+    )(*args)
+    users = jnp.concatenate([features, meta], axis=0)
+    items = own_items
+    item_slots = [items, *gather_slots(own_items, peers, early=(3,))[1:]]
+    user_slots = gather_slots(users, peers, early=(3,))
+    metas = [slot[count:] for slot in user_slots]
+    rows = call(
+        functools.partial(rows_kernel, cap, peers),
+        metas,
+        [jax.ShapeDtypeStruct((8, peers * cap), F32)],
+    )[0]
+    all_rows = [rows]
+    for step in range(1, groups):
+        all_rows.append(to_partner(rows, step, groups))
+    tower = [jax.ShapeDtypeStruct((width, width), F32)] * 2
+    pairs = peers * count
+    state = []
+    for step in range(peers // batch):
+        first = step == 0
+        args = user_slots[step * batch : (step + 1) * batch]
+        args += item_slots if first else [gathered]
+        args += [w_first, w_second, *state]
+        at = len(args) - 4
+        shapes = [
+            jax.ShapeDtypeStruct((pairs, pairs), BF16),
+            jax.ShapeDtypeStruct((width, pairs), BF16),
+            *tower,
+            *[jax.ShapeDtypeStruct((pairs, width), BF16)] * first,
+        ]
+        state = call(
+            functools.partial(group_kernel, batch, peers, step * batch, first),
+            args,
+            shapes,
+            scratch=[pltpu.VMEM((count, pairs), F32) for _ in range(batch)],
+            aliases={} if first else {at + one: one for one in range(4)},
+            flops=6 * batch * peers * count * count * width,
+            limit=16,
+        )
+        if first:
+            *state, gathered = state
+    dscore, vecs, *state = state
+    grad_first, grad_second = sum_towers(*state, groups)
+    sends = []
+    halves = [range(groups // 2, groups), range(groups // 2)]
+    for steps in halves:
+        outs = call(
+            functools.partial(compact_kernel, cap, peers, groups, steps),
+            [dscore, vecs, *metas],
+            [jax.ShapeDtypeStruct((width // groups, peers * cap), BF16)] * len(steps),
+            flops=pairs * pairs * width,
+        )
+        sends = [*outs, *sends]
+    got = [sends[0]]
+    for step in range(1, groups):
+        got.append(to_partner(sends[step], step, groups))
+    table = None
+    turns = [range(groups // 2), *[range(one, one + 1) for one in range(groups // 2, groups)]]
+    for turn, steps in enumerate(turns):
+        args = [*[got[one] for one in steps], *[all_rows[one] for one in steps]]
+        args += [] if turn == 0 else [table]
+        table = call(
+            functools.partial(scatter_kernel, len(steps), turn == 0),
+            args,
+            [jax.ShapeDtypeStruct((width // groups, ITEMS_DEV), F32)],
+        )[0]
+    return grad_first, grad_second, table.T
+
+
+def sharded_group_body(
     user_features, w_first, w_second, item_embed, example_weight, positive, item_owner, item_row
 ):
     features = user_features[0]
@@ -104,6 +476,14 @@
         P("grp", "rows", None),
         P("grp", "rows"),
     )
+
+    def body(*args):
+        count, width = args[3].shape[1:]
+        pairs = count * mesh.shape["rows"]
+        held = pairs * (8 * count + 6 * width)
+        fits = held <= VMEM_BUDGET and count == width == args[0].shape[2] and count <= 256
+        return (whole_group_body if fits else sharded_group_body)(*args)
+
     return jax.shard_map(
         body, mesh=mesh, in_specs=placed, out_specs=(P(), P(), P("rows", "grp")), check_vma=False
     )

time: 302 us -> 72.2 us (0.24)
  waiting for transfers between devices: 183 us -> 18.9 us
  blocking collectives: 55.7 us -> 0 us
  Pallas kernels: 0 us -> 24.9 us
  local copies, waits for them, and re-layouts: 14.9 us -> 0.04 us
  starting transfers between devices: 11.8 us -> 25.5 us
  between operations: 13.9 us -> 0.85 us
  matrix products: 11.7 us -> 0 us
  other arithmetic: 10.6 us -> 1.6 us
    psum x1 -> x0, waiting for transfers between devices: 100 us -> none  [body(): grad_first, grad_second = lax.psum((d_first, d_second), ('rows', 'grp'))]
    all_gather x3 -> x0, blocking collectives: 55.7 us -> none  [the longest x1 21.1 us: body(): lax.all_gather(targets.astype(jnp.float32), 'rows', axis=0, tiled=True)]
    unnamed x5 -> x0, waiting for transfers between devices: 45.5 us -> none
    ppermute x0 -> x23, starting transfers between devices: none -> 25.5 us  [the longest x14 19.3 us: along(): lax.ppermute(value, 'rows', [(one, one ^ bit) for one in range(size)])]
    pallas_call x0 -> x11, Pallas kernels: none -> 24.9 us  [the longest x10 23.5 us: call(): pl.pallas_call(kernel, out_shape=shapes, in_specs=[VMEM] * len(args), out...]
    all_to_all x2 -> x0, waiting for transfers between devices: 20.8 us -> none  [the longest x1 20.8 us: body(): lax.all_to_all(send_grad, 'rows', split_axis=0, concat_axis=0, tiled=True)]
    ppermute x0 -> x23, waiting for transfers between devices: none -> 18.9 us  [the longest x9 11.9 us: to_partner(): return lax.ppermute(value, 'grp', pairs)]
    all_gather x2 -> x0, waiting for transfers between devices: 16.1 us -> none  [the longest x1 16.1 us: body(): everyone = lax.all_gather(user_vecs, 'rows', axis=0, tiled=True)]
  transfers between devices with their start and end apart: 6 -> 23, of which waited for: 4 -> 8; matrix products, arithmetic and copies ran while one was open for 12% -> 1% of each run, Pallas kernels for 0% -> 29%
where the time goes in v1:
time: 72.2 us; the launch traced here: 71.8 us
  starting transfers between devices  25.5 us (35%)
  Pallas kernels  24.9 us (34%)
  waiting for transfers between devices  18.9 us (26%)
  other arithmetic  1.6 us (2%)
  between operations  0.85 us (1%)
    pallas_call x10, Pallas kernels, call(): pl.pallas_call(kernel, out_shape=shapes, in_specs=[VMEM] * len(args), out...  23.5 us
    ppermute x14, starting transfers between devices, along(): lax.ppermute(value, 'rows', [(one, one ^ bit) for one in range(size)])  19.3 us
    ppermute x9, waiting for transfers between devices, to_partner(): return lax.ppermute(value, 'grp', pairs)  11.9 us
    ppermute x14, waiting for transfers between devices, along(): lax.ppermute(value, 'rows', [(one, one ^ bit) for one in range(size)])  7.04 us
    ppermute x9, starting transfers between devices, to_partner(): return lax.ppermute(value, 'grp', pairs)  6.22 us
  transfers between devices with their start and end apart: 23, of which 8 were waited for; matrix products, arithmetic and copies ran while one was open for 1% of the time, Pallas kernels for 29%

profile of v1, /device:TPU:0, one launch (start us, length us, event | category | flops | bytes accessed | tf_op | source)
XLA Modules:
  0.0 71.8 jit_solution(9322956210501856588)
XLA Ops:
  0.6 4.1 %collective-permute-start.7 = (bf16[256,256]{1,0:T(8,128)(2,1)}, bf16[256,256]{1,0:T(8,128)(2,1)S(1)}, u32[]{:S(2)}, u32[]{:S(2)}) collective-permute-start(bf16[256,256]{1,0:T(8,128)(2,1)} %bitcast.4), channel_id=1, source_target_pairs={{0,16},{4,20},{8,24},{12,28},{16,0},{20,4},{24,8},{28,12},{1,17},{... | collective-permute-start | bytes 393224 | tf_op jit(solution)/shard_map/ppermute | solution.py:272
  4.8 1.4 %shard_map.103.refs_2_.refs_0_ = bf16[16,256]{1,0:T(8,128)(2,1)} custom-call(f32[1,256]{1,0:T(1,128)} %weight_hbm.1, s32[1,256]{1,0:T(1,128)} %target_hbm.1, s32[1,256]{1,0:T(1,128)} %bitcast.10, s32[1,256]{1,0:T(1,128)} %row_hbm.1), custom_call_target="tpu_custom_call" | custom-call | flops 8589934592 | bytes 1048576 | tf_op jit(solution)/shard_map/pallas_call | solution.py:312
  7.1 1.8 %collective-permute-start.4 = (bf16[256,256]{1,0:T(8,128)(2,1)S(1)}, bf16[256,256]{1,0:T(8,128)(2,1)S(1)}, u32[]{:S(2)}, u32[]{:S(2)}) collective-permute-start(bf16[256,256]{1,0:T(8,128)(2,1)S(1)} %bitcast.5), channel_id=1, source_target_pairs={{0,4},{4,0},{8,12},{12,8},{16,20},{20,16},{24,28},{28,24},{1,5},{5... | collective-permute-start | bytes 393224 | tf_op jit(solution)/shard_map/ppermute | solution.py:272
  8.8 1.6 %collective-permute-start.5 = (bf16[256,256]{1,0:T(8,128)(2,1)S(1)}, bf16[256,256]{1,0:T(8,128)(2,1)S(1)}, u32[]{:S(2)}, u32[]{:S(2)}) collective-permute-start(bf16[256,256]{1,0:T(8,128)(2,1)S(1)} %bitcast.6), channel_id=1, source_target_pairs={{0,8},{4,12},{8,0},{12,4},{16,24},{20,28},{24,16},{28,20},{1,9},{5... | collective-permute-start | bytes 393224 | tf_op jit(solution)/shard_map/ppermute | solution.py:272
  10.4 4.3 %collective-permute-done.7.refs_6_ = bf16[256,256]{1,0:T(8,128)(2,1)S(1)} collective-permute-done((bf16[256,256]{1,0:T(8,128)(2,1)}, bf16[256,256]{1,0:T(8,128)(2,1)S(1)}, u32[]{:S(2)}, u32[]{:S(2)}) %collective-permute-start.7) | collective-permute-done | bytes 131104 | tf_op jit(solution)/shard_map/ppermute | solution.py:272
  15.2 1.7 %collective-permute-start.3 = (bf16[272,256]{1,0:T(8,128)(2,1)S(1)}, bf16[272,256]{1,0:T(8,128)(2,1)S(1)}, u32[]{:S(2)}, u32[]{:S(2)}) collective-permute-start(bf16[272,256]{1,0:T(8,128)(2,1)S(1)} %pad_maximum_fusion.refs_0_), channel_id=1, source_target_pairs={{0,4},{4,0},{8,12},{12,8},{16,20},{20,16},{24,28},{28,24},{1,5},{5... | collective-permute-start | bytes 417800 | tf_op jit(solution)/shard_map/ppermute | solution.py:272
  17.3 1.6 %collective-permute-start.1 = (bf16[272,256]{1,0:T(8,128)(2,1)S(1)}, bf16[272,256]{1,0:T(8,128)(2,1)S(1)}, u32[]{:S(2)}, u32[]{:S(2)}) collective-permute-start(bf16[272,256]{1,0:T(8,128)(2,1)S(1)} %collective-permute-done.refs_0_), channel_id=1, source_target_pairs={{0,8},{4,12},{8,0},{12,4},{16,24},{20,28},{24,16},{28,20},{1,9},{5... | collective-permute-start | bytes 417800 | tf_op jit(solution)/shard_map/ppermute | solution.py:272
  19.5 1.5 %collective-permute-start.6 = (bf16[256,256]{1,0:T(8,128)(2,1)S(1)}, bf16[256,256]{1,0:T(8,128)(2,1)S(1)}, u32[]{:S(2)}, u32[]{:S(2)}) collective-permute-start(bf16[256,256]{1,0:T(8,128)(2,1)S(1)} %collective-permute-done.4.refs_3_), channel_id=1, source_target_pairs={{0,8},{4,12},{8,0},{12,4},{16,24},{20,28},{24,16},{28,20},{1,9},{5... | collective-permute-start | bytes 393224 | tf_op jit(solution)/shard_map/ppermute | solution.py:272
  21.0 2.3 %collective-permute-start.10 = (bf16[256,256]{1,0:T(8,128)(2,1)S(1)}, bf16[256,256]{1,0:T(8,128)(2,1)S(1)}, u32[]{:S(2)}, u32[]{:S(2)}) collective-permute-start(bf16[256,256]{1,0:T(8,128)(2,1)S(1)} %collective-permute-done.9.refs_8_), channel_id=1, source_target_pairs={{0,4},{4,0},{8,12},{12,8},{16,20},{20,16},{24,28},{28,24},{1,5},{5... | collective-permute-start | bytes 393224 | tf_op jit(solution)/shard_map/ppermute | solution.py:272
  23.3 1.3 %collective-permute-done.8.refs_7_ = bf16[256,256]{1,0:T(8,128)(2,1)S(1)} collective-permute-done((bf16[256,256]{1,0:T(8,128)(2,1)S(1)}, bf16[256,256]{1,0:T(8,128)(2,1)S(1)}, u32[]{:S(2)}, u32[]{:S(2)}) %collective-permute-start.8) | collective-permute-done | bytes 131104 | tf_op jit(solution)/shard_map/ppermute | solution.py:272
  26.8 1.5 %collective-permute-start.13 = (bf16[272,256]{1,0:T(8,128)(2,1)S(1)}, bf16[272,256]{1,0:T(8,128)(2,1)S(1)}, u32[]{:S(2)}, u32[]{:S(2)}) collective-permute-start(bf16[272,256]{1,0:T(8,128)(2,1)S(1)} %collective-permute-done.3.refs_1_), channel_id=1, source_target_pairs={{0,8},{4,12},{8,0},{12,4},{16,24},{20,28},{24,16},{28,20},{1,9},{5... | collective-permute-start | bytes 417800 | tf_op jit(solution)/shard_map/ppermute | solution.py:272
  29.1 3.7 %shard_map.104 = (bf16[2048,2048]{1,0:T(8,128)(2,1)S(1)}, bf16[256,2048]{1,0:T(8,128)(2,1)S(1)}, f32[256,256]{1,0:T(8,128)S(1)}, f32[256,256]{1,0:T(8,128)S(1)}, bf16[2048,256]{1,0:T(8,128)(2,1)S(1)}) custom-call(bf16[272,256]{1,0:T(8,128)(2,1)S(1)} %pad_maximum_fusion.refs_0_, bf16[272,256]{1,0:T(8,128)(2,1)S(1)} %collective-permute-done.3.refs_1_, ...), custom_call_target="tpu_custom_call" | custom-call | flops 1610612736 | bytes 1048576 | tf_op jit(solution)/shard_map/pallas_call | solution.py:245
  32.9 3.8 %shard_map.105 = (bf16[2048,2048]{1,0:T(8,128)(2,1)S(1)}, bf16[256,2048]{1,0:T(8,128)(2,1)S(1)}, f32[256,256]{1,0:T(8,128)S(1)}, f32[256,256]{1,0:T(8,128)S(1)}) custom-call(bf16[272,256]{1,0:T(8,128)(2,1)S(1)} %collective-permute-done.12.refs_0_, ...), custom_call_target="tpu_custom_call", output_to_operand_aliasing={{0}: (5, {}), {1}: (6, {}), {2}: (7, {}), {3}: (8, {})} | custom-call | flops 1610612736 | bytes 1048576 | tf_op jit(solution)/shard_map/pallas_call | solution.py:245
  36.7 3.8 %shard_map.106 = (bf16[2048,2048]{1,0:T(8,128)(2,1)S(1)}, bf16[256,2048]{1,0:T(8,128)(2,1)S(1)}, f32[256,256]{1,0:T(8,128)S(1)}, f32[256,256]{1,0:T(8,128)S(1)}) custom-call(bf16[272,256]{1,0:T(8,128)(2,1)S(1)} %collective-permute-done.refs_0_, ...), custom_call_target="tpu_custom_call", output_to_operand_aliasing={{0}: (5, {}), {1}: (6, {}), {2}: (7, {}), {3}: (8, {})} | custom-call | flops 1610612736 | bytes 1048576 | tf_op jit(solution)/shard_map/pallas_call | solution.py:245
  40.5 4.0 %shard_map.107 = (bf16[2048,2048]{1,0:T(8,128)(2,1)S(1)}, bf16[256,2048]{1,0:T(8,128)(2,1)S(1)}, f32[256,256]{1,0:T(8,128)S(1)}, f32[256,256]{1,0:T(8,128)S(1)}) custom-call(bf16[272,256]{1,0:T(8,128)(2,1)S(1)} %collective-permute-done.1.refs_0_, ...), custom_call_target="tpu_custom_call", output_to_operand_aliasing={{0}: (5, {}), {1}: (6, {}), {2}: (7, {}), {3}: (8, {})} | custom-call | flops 1610612736 | bytes 1048576 | tf_op jit(solution)/shard_map/pallas_call | solution.py:245
  44.5 1.5 %collective-permute-done.14 = f32[256,256]{1,0:T(8,128)S(1)} collective-permute-done((f32[256,256]{1,0:T(8,128)S(1)}, f32[256,256]{1,0:T(8,128)S(1)}, u32[]{:S(2)}, u32[]{:S(2)}) %collective-permute-start.14) | collective-permute-done | bytes 262176 | tf_op jit(solution)/shard_map/ppermute | solution.py:268
  46.1 1.6 %collective-permute-start.15 = (f32[256,256]{1,0:T(8,128)S(1)}, f32[256,256]{1,0:T(8,128)S(1)}, u32[]{:S(2)}, u32[]{:S(2)}) collective-permute-start(f32[256,256]{1,0:T(8,128)S(1)} %add.11), channel_id=1, source_target_pairs={{0,2},{1,3},{2,0},{3,1},{4,6},{5,7},{6,4},{7,5},{8,10},{9,11},{10,... | collective-permute-start | bytes 786440 | tf_op jit(solution)/shard_map/ppermute | solution.py:268
  47.7 6.8 %collective-permute-done.15 = f32[256,256]{1,0:T(8,128)S(1)} collective-permute-done((f32[256,256]{1,0:T(8,128)S(1)}, f32[256,256]{1,0:T(8,128)S(1)}, u32[]{:S(2)}, u32[]{:S(2)}) %collective-permute-start.15) | collective-permute-done | bytes 262176 | tf_op jit(solution)/shard_map/ppermute | solution.py:268
  54.6 2.0 %shard_map.110 = (bf16[64,1024]{1,0:T(8,128)(2,1)S(1)}, bf16[64,1024]{1,0:T(8,128)(2,1)S(1)}) custom-call(bf16[2048,2048]{1,0:T(8,128)(2,1)S(1)} %get-tuple-element.39.refs_0_, bf16[256,2048]{1,0:T(8,128)(2,1)S(1)} %get-tuple-element.40.refs_1_, bf16[16,256]{1,0:T(8,128)(2,1)S(1)} %copy-done.2, bf16[16,256]{1,0:T(8,128)(2,1)S(1)} %slice.28.refs_3_.refs_1_, ...), custom_call_target="tpu_custom_call" | custom-call | flops 1073741824 | bytes 1048576 | tf_op jit(solution)/shard_map/pallas_call | solution.py:245
  57.2 2.0 %shard_map.108 = (bf16[64,1024]{1,0:T(8,128)(2,1)S(1)}, bf16[64,1024]{1,0:T(8,128)(2,1)S(1)}) custom-call(bf16[2048,2048]{1,0:T(8,128)(2,1)S(1)} %get-tuple-element.39.refs_0_, bf16[256,2048]{1,0:T(8,128)(2,1)S(1)} %get-tuple-element.40.refs_1_, bf16[16,256]{1,0:T(8,128)(2,1)S(1)} %copy-done.2, bf16[16,256]{1,0:T(8,128)(2,1)S(1)} %slice.28.refs_3_.refs_1_, ...), custom_call_target="tpu_custom_call" | custom-call | flops 1073741824 | bytes 1048576 | tf_op jit(solution)/shard_map/pallas_call | solution.py:245
  59.1 1.6 %collective-permute-start.19 = (bf16[64,1024]{1,0:T(8,128)(2,1)S(1)}, bf16[64,1024]{1,0:T(8,128)(2,1)S(1)}, u32[]{:S(2)}, u32[]{:S(2)}) collective-permute-start(bf16[64,1024]{1,0:T(8,128)(2,1)S(1)} %get-tuple-element.42), channel_id=1, source_target_pairs={{0,2},{1,3},{2,0},{3,1},{4,6},{5,7},{6,4},{7,5},{8,10},{9,11},{10,... | collective-permute-start | bytes 393224 | tf_op jit(solution)/shard_map/ppermute | solution.py:268
  62.8 1.5 %collective-permute-start.20 = (f32[8,1024]{1,0:T(8,128)S(1)}, f32[8,1024]{1,0:T(8,128)S(1)}, u32[]{:S(2)}, u32[]{:S(2)}) collective-permute-start(f32[8,1024]{1,0:T(8,128)S(1)} %shard_map.109.refs_2_), channel_id=1, source_target_pairs={{0,2},{1,3},{2,0},{3,1},{4,6},{5,7},{6,4},{7,5},{8,10},{9,11},{10,... | collective-permute-start | bytes 98312 | tf_op jit(solution)/shard_map/ppermute | solution.py:268
  65.8 2.7 %collective-permute-done.20.refs_1_ = f32[8,1024]{1,0:T(8,128)S(1)} collective-permute-done((f32[8,1024]{1,0:T(8,128)S(1)}, f32[8,1024]{1,0:T(8,128)S(1)}, u32[]{:S(2)}, u32[]{:S(2)}) %collective-permute-start.20) | collective-permute-done | bytes 32800 | tf_op jit(solution)/shard_map/ppermute | solution.py:268
  69.3 1.7 %shard_map.113 = f32[64,4096]{1,0:T(8,128)} custom-call(bf16[64,1024]{1,0:T(8,128)(2,1)S(1)} %collective-permute-done.17.refs_0_, f32[8,1024]{1,0:T(8,128)S(1)} %collective-permute-done.18.refs_1_, f32[64,4096]{1,0:T(8,128)S(1)} %shard_map.112.refs_2_), custom_call_target="tpu_custom_call" | custom-call | flops 1048576 | bytes 1048576 | tf_op jit(solution)/shard_map/pallas_call | solution.py:245
  (54 shorter events, 11.1 us)
Async XLA Ops:
  0.6 14.1 %collective-permute-start.7 = (bf16[256,256]{1,0:T(8,128)(2,1)}, bf16[256,256]{1,0:T(8,128)(2,1)S(1)}, u32[]{:S(2)}, u32[]{:S(2)}) collective-permute-start(bf16[256,256]{1,0:T(8,128)(2,1)} %bitcast.4), channel_id=1, source_target_pairs={{0,16},{4,20},{8,24},{12,28},{16,0},{20,4},{24,8},{28,12},{1,17},{... | collective-permute-start | bytes 393224 | tf_op jit(solution)/shard_map/ppermute | solution.py:272
  4.8 24.4 %copy-start.1 = (bf16[256,256]{1,0:T(8,128)(2,1)S(1)}, bf16[256,256]{1,0:T(8,128)(2,1)}, u32[]{:S(2)}) copy-start(bf16[256,256]{1,0:T(8,128)(2,1)} %refs_4_.5) | copy-start | bytes 393220
  6.9 10.4 %collective-permute-start = (bf16[272,256]{1,0:T(8,128)(2,1)S(1)}, bf16[272,256]{1,0:T(8,128)(2,1)S(1)}, u32[]{:S(2)}, u32[]{:S(2)}) collective-permute-start(bf16[272,256]{1,0:T(8,128)(2,1)S(1)} %pad_maximum_fusion.refs_0_), channel_id=1, source_target_pairs={{0,16},{4,20},{8,24},{12,28},{16,0},{20,4},{24,8},{28,12},{1,17},{... | collective-permute-start | bytes 417800 | tf_op jit(solution)/shard_map/ppermute | solution.py:272
  7.1 11.9 %collective-permute-start.4 = (bf16[256,256]{1,0:T(8,128)(2,1)S(1)}, bf16[256,256]{1,0:T(8,128)(2,1)S(1)}, u32[]{:S(2)}, u32[]{:S(2)}) collective-permute-start(bf16[256,256]{1,0:T(8,128)(2,1)S(1)} %bitcast.5), channel_id=1, source_target_pairs={{0,4},{4,0},{8,12},{12,8},{16,20},{20,16},{24,28},{28,24},{1,5},{5... | collective-permute-start | bytes 393224 | tf_op jit(solution)/shard_map/ppermute | solution.py:272
  8.8 10.7 %collective-permute-start.5 = (bf16[256,256]{1,0:T(8,128)(2,1)S(1)}, bf16[256,256]{1,0:T(8,128)(2,1)S(1)}, u32[]{:S(2)}, u32[]{:S(2)}) collective-permute-start(bf16[256,256]{1,0:T(8,128)(2,1)S(1)} %bitcast.6), channel_id=1, source_target_pairs={{0,8},{4,12},{8,0},{12,4},{16,24},{20,28},{24,16},{28,20},{1,9},{5... | collective-permute-start | bytes 393224 | tf_op jit(solution)/shard_map/ppermute | solution.py:272
  14.8 6.3 %collective-permute-start.9 = (bf16[256,256]{1,0:T(8,128)(2,1)S(1)}, bf16[256,256]{1,0:T(8,128)(2,1)S(1)}, u32[]{:S(2)}, u32[]{:S(2)}) collective-permute-start(bf16[256,256]{1,0:T(8,128)(2,1)S(1)} %collective-permute-done.7.refs_6_), channel_id=1, source_target_pairs={{0,8},{4,12},{8,0},{12,4},{16,24},{20,28},{24,16},{28,20},{1,9},{5... | collective-permute-start | bytes 393224 | tf_op jit(solution)/shard_map/ppermute | solution.py:272
  15.2 8.1 %collective-permute-start.3 = (bf16[272,256]{1,0:T(8,128)(2,1)S(1)}, bf16[272,256]{1,0:T(8,128)(2,1)S(1)}, u32[]{:S(2)}, u32[]{:S(2)}) collective-permute-start(bf16[272,256]{1,0:T(8,128)(2,1)S(1)} %pad_maximum_fusion.refs_0_), channel_id=1, source_target_pairs={{0,4},{4,0},{8,12},{12,8},{16,20},{20,16},{24,28},{28,24},{1,5},{5... | collective-permute-start | bytes 417800 | tf_op jit(solution)/shard_map/ppermute | solution.py:272
  17.3 11.0 %collective-permute-start.1 = (bf16[272,256]{1,0:T(8,128)(2,1)S(1)}, bf16[272,256]{1,0:T(8,128)(2,1)S(1)}, u32[]{:S(2)}, u32[]{:S(2)}) collective-permute-start(bf16[272,256]{1,0:T(8,128)(2,1)S(1)} %collective-permute-done.refs_0_), channel_id=1, source_target_pairs={{0,8},{4,12},{8,0},{12,4},{16,24},{20,28},{24,16},{28,20},{1,9},{5... | collective-permute-start | bytes 417800 | tf_op jit(solution)/shard_map/ppermute | solution.py:272
  19.0 5.7 %collective-permute-start.8 = (bf16[256,256]{1,0:T(8,128)(2,1)S(1)}, bf16[256,256]{1,0:T(8,128)(2,1)S(1)}, u32[]{:S(2)}, u32[]{:S(2)}) collective-permute-start(bf16[256,256]{1,0:T(8,128)(2,1)S(1)} %collective-permute-done.7.refs_6_), channel_id=1, source_target_pairs={{0,4},{4,0},{8,12},{12,8},{16,20},{20,16},{24,28},{28,24},{1,5},{5... | collective-permute-start | bytes 393224 | tf_op jit(solution)/shard_map/ppermute | solution.py:272
  19.5 7.3 %collective-permute-start.6 = (bf16[256,256]{1,0:T(8,128)(2,1)S(1)}, bf16[256,256]{1,0:T(8,128)(2,1)S(1)}, u32[]{:S(2)}, u32[]{:S(2)}) collective-permute-start(bf16[256,256]{1,0:T(8,128)(2,1)S(1)} %collective-permute-done.4.refs_3_), channel_id=1, source_target_pairs={{0,8},{4,12},{8,0},{12,4},{16,24},{20,28},{24,16},{28,20},{1,9},{5... | collective-permute-start | bytes 393224 | tf_op jit(solution)/shard_map/ppermute | solution.py:272
  21.0 8.1 %collective-permute-start.10 = (bf16[256,256]{1,0:T(8,128)(2,1)S(1)}, bf16[256,256]{1,0:T(8,128)(2,1)S(1)}, u32[]{:S(2)}, u32[]{:S(2)}) collective-permute-start(bf16[256,256]{1,0:T(8,128)(2,1)S(1)} %collective-permute-done.9.refs_8_), channel_id=1, source_target_pairs={{0,4},{4,0},{8,12},{12,8},{16,20},{20,16},{24,28},{28,24},{1,5},{5... | collective-permute-start | bytes 393224 | tf_op jit(solution)/shard_map/ppermute | solution.py:272
  23.3 9.6 %collective-permute-start.12 = (bf16[272,256]{1,0:T(8,128)(2,1)S(1)}, bf16[272,256]{1,0:T(8,128)(2,1)S(1)}, u32[]{:S(2)}, u32[]{:S(2)}) collective-permute-start(bf16[272,256]{1,0:T(8,128)(2,1)S(1)} %pad_maximum_fusion.refs_0_), channel_id=1, source_target_pairs={{0,8},{4,12},{8,0},{12,4},{16,24},{20,28},{24,16},{28,20},{1,9},{5... | collective-permute-start | bytes 417800 | tf_op jit(solution)/shard_map/ppermute | solution.py:272
  24.7 12.0 %collective-permute-start.11 = (bf16[272,256]{1,0:T(8,128)(2,1)S(1)}, bf16[272,256]{1,0:T(8,128)(2,1)S(1)}, u32[]{:S(2)}, u32[]{:S(2)}) collective-permute-start(bf16[272,256]{1,0:T(8,128)(2,1)S(1)} %collective-permute-done.refs_0_), channel_id=1, source_target_pairs={{0,4},{4,0},{8,12},{12,8},{16,20},{20,16},{24,28},{28,24},{1,5},{5... | collective-permute-start | bytes 417800 | tf_op jit(solution)/shard_map/ppermute | solution.py:272
  26.8 6.1 %collective-permute-start.13 = (bf16[272,256]{1,0:T(8,128)(2,1)S(1)}, bf16[272,256]{1,0:T(8,128)(2,1)S(1)}, u32[]{:S(2)}, u32[]{:S(2)}) collective-permute-start(bf16[272,256]{1,0:T(8,128)(2,1)S(1)} %collective-permute-done.3.refs_1_), channel_id=1, source_target_pairs={{0,8},{4,12},{8,0},{12,4},{16,24},{20,28},{24,16},{28,20},{1,9},{5... | collective-permute-start | bytes 417800 | tf_op jit(solution)/shard_map/ppermute | solution.py:272
  28.4 12.1 %collective-permute-start.2 = (bf16[272,256]{1,0:T(8,128)(2,1)S(1)}, bf16[272,256]{1,0:T(8,128)(2,1)S(1)}, u32[]{:S(2)}, u32[]{:S(2)}) collective-permute-start(bf16[272,256]{1,0:T(8,128)(2,1)S(1)} %collective-permute-done.1.refs_0_), channel_id=1, source_target_pairs={{0,4},{4,0},{8,12},{12,8},{16,20},{20,16},{24,28},{28,24},{1,5},{5... | collective-permute-start | bytes 417800 | tf_op jit(solution)/shard_map/ppermute | solution.py:272
  44.5 1.6 %collective-permute-start.14 = (f32[256,256]{1,0:T(8,128)S(1)}, f32[256,256]{1,0:T(8,128)S(1)}, u32[]{:S(2)}, u32[]{:S(2)}) collective-permute-start(f32[256,256]{1,0:T(8,128)S(1)} %get-tuple-element.38), channel_id=1, source_target_pairs={{0,1},{1,0},{2,3},{3,2},{4,5},{5,4},{6,7},{7,6},{8,9},{9,8},{10,11... | collective-permute-start | bytes 786440 | tf_op jit(solution)/shard_map/ppermute | solution.py:268
  46.1 8.4 %collective-permute-start.15 = (f32[256,256]{1,0:T(8,128)S(1)}, f32[256,256]{1,0:T(8,128)S(1)}, u32[]{:S(2)}, u32[]{:S(2)}) collective-permute-start(f32[256,256]{1,0:T(8,128)S(1)} %add.11), channel_id=1, source_target_pairs={{0,2},{1,3},{2,0},{3,1},{4,6},{5,7},{6,4},{7,5},{8,10},{9,11},{10,... | collective-permute-start | bytes 786440 | tf_op jit(solution)/shard_map/ppermute | solution.py:268
  54.5 16.5 %collective-permute-start.16 = (f32[256,256]{1,0:T(8,128)S(1)}, f32[256,256]{1,0:T(8,128)S(1)}, u32[]{:S(2)}, u32[]{:S(2)}) collective-permute-start(f32[256,256]{1,0:T(8,128)S(1)} %add.12), channel_id=1, source_target_pairs={{0,1},{1,0},{2,3},{3,2},{4,5},{5,4},{6,7},{7,6},{8,9},{9,8},{10,11... | collective-permute-start | bytes 786440 | tf_op jit(solution)/shard_map/ppermute | solution.py:268
  56.6 7.7 %collective-permute-start.21 = (bf16[64,1024]{1,0:T(8,128)(2,1)S(1)}, bf16[64,1024]{1,0:T(8,128)(2,1)S(1)}, u32[]{:S(2)}, u32[]{:S(2)}) collective-permute-start(bf16[64,1024]{1,0:T(8,128)(2,1)S(1)} %get-tuple-element.44), channel_id=1, source_target_pairs={{0,1},{1,0},{2,3},{3,2},{4,5},{5,4},{6,7},{7,6},{8,9},{9,8},{10,11... | collective-permute-start | bytes 393224 | tf_op jit(solution)/shard_map/ppermute | solution.py:268
  59.1 9.4 %collective-permute-start.19 = (bf16[64,1024]{1,0:T(8,128)(2,1)S(1)}, bf16[64,1024]{1,0:T(8,128)(2,1)S(1)}, u32[]{:S(2)}, u32[]{:S(2)}) collective-permute-start(bf16[64,1024]{1,0:T(8,128)(2,1)S(1)} %get-tuple-element.42), channel_id=1, source_target_pairs={{0,2},{1,3},{2,0},{3,1},{4,6},{5,7},{6,4},{7,5},{8,10},{9,11},{10,... | collective-permute-start | bytes 393224 | tf_op jit(solution)/shard_map/ppermute | solution.py:268
  60.7 8.5 %collective-permute-start.17 = (bf16[64,1024]{1,0:T(8,128)(2,1)S(1)}, bf16[64,1024]{1,0:T(8,128)(2,1)S(1)}, u32[]{:S(2)}, u32[]{:S(2)}) collective-permute-start(bf16[64,1024]{1,0:T(8,128)(2,1)S(1)} %get-tuple-element.41), channel_id=1, source_target_pairs={{0,3},{1,2},{2,1},{3,0},{4,7},{5,6},{6,5},{7,4},{8,11},{9,10},{10,... | collective-permute-start | bytes 393224 | tf_op jit(solution)/shard_map/ppermute | solution.py:268
  61.3 1.5 %collective-permute-start.22 = (f32[8,1024]{1,0:T(8,128)S(1)}, f32[8,1024]{1,0:T(8,128)S(1)}, u32[]{:S(2)}, u32[]{:S(2)}) collective-permute-start(f32[8,1024]{1,0:T(8,128)S(1)} %shard_map.109.refs_2_), channel_id=1, source_target_pairs={{0,1},{1,0},{2,3},{3,2},{4,5},{5,4},{6,7},{7,6},{8,9},{9,8},{10,11... | collective-permute-start | bytes 98312 | tf_op jit(solution)/shard_map/ppermute | solution.py:268
  62.8 5.7 %collective-permute-start.20 = (f32[8,1024]{1,0:T(8,128)S(1)}, f32[8,1024]{1,0:T(8,128)S(1)}, u32[]{:S(2)}, u32[]{:S(2)}) collective-permute-start(f32[8,1024]{1,0:T(8,128)S(1)} %shard_map.109.refs_2_), channel_id=1, source_target_pairs={{0,2},{1,3},{2,0},{3,1},{4,6},{5,7},{6,4},{7,5},{8,10},{9,11},{10,... | collective-permute-start | bytes 98312 | tf_op jit(solution)/shard_map/ppermute | solution.py:268
  64.3 5.0 %collective-permute-start.18 = (f32[8,1024]{1,0:T(8,128)S(1)}, f32[8,1024]{1,0:T(8,128)S(1)}, u32[]{:S(2)}, u32[]{:S(2)}) collective-permute-start(f32[8,1024]{1,0:T(8,128)S(1)} %shard_map.109.refs_2_), channel_id=1, source_target_pairs={{0,3},{1,2},{2,1},{3,0},{4,7},{5,6},{6,5},{7,4},{8,11},{9,10},{10,... | collective-permute-start | bytes 98312 | tf_op jit(solution)/shard_map/ppermute | solution.py:268
  (4 other events, 42.3 us)

commit v2 on v1

--- a/solution.py
+++ b/solution.py
@@ -59,7 +59,7 @@
     meta_ref[...] = stack_rows([*rows, high, middle, low], weight.shape[1])
 
 
-def group_kernel(users, slots, begin, first, *refs):
+def group_kernel(users, slots, begin, first, last, *refs):
     user_refs, refs = refs[:users], refs[users:]
     if first:
         item_refs, refs = refs[:slots], refs[slots:]
@@ -74,7 +74,7 @@
     refs = refs[4:]
     if first:
         items_ref, refs = refs[0], refs[1:]
-    scores_refs = refs
+    scores_ref, slopes_ref, hidden_ref, sums_ref = refs
     count = user_refs[0].shape[0] - META
     lanes = 128
     tall = 16
@@ -86,12 +86,15 @@
     w_first = first_ref[...]
     w_second = second_ref[...]
     lane = lax.broadcasted_iota(jnp.int32, (tall, lanes), 1)
+    lines = count // tall
+    stride = max(1, lines // slots)
 
     def span(slot):
         return slice(slot * count, (slot + 1) * count)
 
-    state = []
-    for user in range(users):
+    state = [None] * users
+
+    def enter(user):
         features = user_refs[user][0:count, :]
         meta = jnp.transpose(user_refs[user][count : count + META, :].astype(F32))
         weight = meta[:, 5:6] + meta[:, 6:7] + meta[:, 7:8]
@@ -99,19 +102,22 @@
         pre_act = dot_nn(features, w_first)
         gate = jax.nn.sigmoid(pre_act)
         hidden = (pre_act * gate).astype(BF16)
+        slopes_ref[user % 3] = gate * (1.0 + pre_act * (1.0 - gate))
+        hidden_ref[user % 3] = hidden
         vecs = dot_nn(hidden, w_second).astype(BF16)
         vecs_ref[:, span(begin + user)] = jnp.transpose(vecs)
-        state.append((weight, target, hidden, vecs))
+        state[user] = [weight, target, vecs, None]
 
     def score(user, slot):
-        scores_refs[user][:, span(slot)] = contract_last(state[user][3], items_ref[span(slot), :])
+        part = contract_last(state[user][2], items_ref[span(slot), :])
+        scores_ref[user % 2, :, span(slot)] = part
 
     def soften(user, line):
         rows = slice(line * tall, (line + 1) * tall)
         weight = state[user][0][rows]
         away = lane - state[user][1][rows]
         total_lanes = slots * count
-        parts = [scores_refs[user][rows, at : at + lanes] for at in range(0, total_lanes, lanes)]
+        parts = [scores_ref[user % 2, rows, at : at + lanes] for at in range(0, total_lanes, lanes)]
         top = parts[0]
         for part in parts[1:]:
             top = jnp.maximum(top, part)
@@ -129,39 +135,41 @@
             out = slice((begin + user) * count + line * tall, (begin + user) * count + (line + 1) * tall)
             dscore_ref[out, start : start + lanes] = part.astype(BF16)
 
-    def pull(user):
-        hidden = state[user][2]
+    def pull(user, piece):
+        one = state[user]
+        rows = span(begin + user)
         half = slots * count // 2
-        grad_user = dot_nn(dscore_ref[span(begin + user), :half], items_ref[:half, :])
-        grad_user += dot_nn(dscore_ref[span(begin + user), half:], items_ref[half:, :])
-        grad_user = grad_user.astype(BF16)
-        d_second = contract_first(hidden, grad_user)
-        back = contract_last(grad_user, w_second)
-        features = user_refs[user][0:count, :]
-        pre_act = dot_nn(features, w_first)
-        gate = jax.nn.sigmoid(pre_act)
-        grad_pre = back * gate * (1.0 + pre_act * (1.0 - gate))
-        d_first = contract_first(features, grad_pre.astype(BF16))
-        return d_first, d_second
-
-    lines = count // tall
-    for slot in range(slots):
-        score(0, slot)
-    for user in range(users):
+        if piece == 0:
+            one[3] = dot_nn(dscore_ref[rows, :half], items_ref[:half, :])
+        elif piece == 1:
+            one[3] = (one[3] + dot_nn(dscore_ref[rows, half:], items_ref[half:, :])).astype(BF16)
+        elif piece == 2:
+            keep(second_sum, 1, user, contract_first(hidden_ref[user % 3], one[3]))
+            one[3] = contract_last(one[3], w_second)
+        else:
+            grad_pre = (one[3] * slopes_ref[user % 3]).astype(BF16)
+            keep(first_sum, 0, user, contract_first(user_refs[user][0:count, :], grad_pre))
+
+    def keep(ref, index, user, value):
+        if user:
+            ref[...] += value
+        else:
+            ref[...] = value if first else (mine_in, other_in)[index][...] + value
+
+    first_sum, second_sum = (mine_ref, other_ref) if not last else (sums_ref.at[0], sums_ref.at[1])
+    for step in range(users + 2):
+        if step < users:
+            enter(step)
         for line in range(lines):
-            soften(user, line)
-            if user + 1 < users and line % (lines // slots) == 0:
-                score(user + 1, line // (lines // slots))
-    for user in range(users):
-        d_first, d_second = pull(user)
-        mine = jnp.where(flip, d_second, d_first)
-        other = jnp.where(flip, d_first, d_second)
-        if user:
-            mine_ref[...] += mine
-            other_ref[...] += other
-        else:
-            mine_ref[...] = mine if first else mine_in[...] + mine
-            other_ref[...] = other if first else other_in[...] + other
+            if step < users and line % stride == 0 and line // stride < slots:
+                score(step, line // stride)
+            if 1 <= step <= users:
+                soften(step - 1, line)
+            if 2 <= step and line % (lines // 4) == 0:
+                pull(step - 2, line // (lines // 4))
+    if last:
+        mine_ref[...] = jnp.where(flip, sums_ref[1], sums_ref[0])
+        other_ref[...] = jnp.where(flip, sums_ref[0], sums_ref[1])
 
 
 def select_slots(meta_refs, cap):
@@ -182,21 +190,17 @@
     return picks
 
 
-def rows_kernel(cap, slots, *refs):
-    metas, rows_ref = refs[:slots], refs[slots]
-    picks = select_slots(metas, cap)
-    for slot in range(slots):
-        digits = contract_last(metas[slot][...], picks[slot])
-        ones = contract_last(jnp.ones((META, picks[slot].shape[1]), BF16), picks[slot])
-        row = digits[1:2] * 256.0 + digits[2:3]
-        row = jnp.where(ones[0:1] > 0.5, row, -1.0)
-        rows_ref[:, slot * cap : (slot + 1) * cap] = jnp.broadcast_to(row, (8, cap))
-
-
 def compact_kernel(cap, slots, groups, steps, *refs):
     dscore_ref, vecs_ref, refs = refs[0], refs[1], refs[2:]
     metas, outs = refs[:slots], refs[slots:]
     picks = select_slots(metas, cap)
+    if len(outs) > len(steps):
+        for slot in range(slots):
+            digits = contract_last(metas[slot][...], picks[slot])
+            ones = contract_last(jnp.ones((META, picks[slot].shape[1]), BF16), picks[slot])
+            row = digits[1:2] * 256.0 + digits[2:3]
+            row = jnp.where(ones[0:1] > 0.5, row, -1.0)
+            outs[-1][:, slot * cap : (slot + 1) * cap] = row
     count = metas[0].shape[1]
     width = vecs_ref.shape[0] // groups
     me = lax.axis_index("grp")
@@ -272,12 +276,12 @@
     return lax.ppermute(value, "rows", [(one, one ^ bit) for one in range(size)])
 
 
-def gather_slots(own, size, early=()):
+def gather_slots(own, size):
     slots = [own]
     for slot in range(1, size):
         bit = slot & -slot
-        if slot in early:
-            bit = 1 << (slot.bit_length() - 1)
+        if slot == 3:
+            bit = 2
         slots.append(along(slots[slot ^ bit], bit, size))
     return slots
 
@@ -325,17 +329,9 @@
     )(*args)
     users = jnp.concatenate([features, meta], axis=0)
     items = own_items
-    item_slots = [items, *gather_slots(own_items, peers, early=(3,))[1:]]
-    user_slots = gather_slots(users, peers, early=(3,))
+    item_slots = [items, *gather_slots(own_items, peers)[1:]]
+    user_slots = gather_slots(users, peers)
     metas = [slot[count:] for slot in user_slots]
-    rows = call(
-        functools.partial(rows_kernel, cap, peers),
-        metas,
-        [jax.ShapeDtypeStruct((8, peers * cap), F32)],
-    )[0]
-    all_rows = [rows]
-    for step in range(1, groups):
-        all_rows.append(to_partner(rows, step, groups))
     tower = [jax.ShapeDtypeStruct((width, width), F32)] * 2
     pairs = peers * count
     state = []
@@ -352,10 +348,15 @@
             *[jax.ShapeDtypeStruct((pairs, width), BF16)] * first,
         ]
         state = call(
-            functools.partial(group_kernel, batch, peers, step * batch, first),
+            functools.partial(group_kernel, batch, peers, step * batch, first, (step + 1) * batch == peers),
             args,
             shapes,
-            scratch=[pltpu.VMEM((count, pairs), F32) for _ in range(batch)],
+            scratch=[
+                pltpu.VMEM((2, count, pairs), F32),
+                pltpu.VMEM((3, count, width), F32),
+                pltpu.VMEM((3, count, width), BF16),
+                pltpu.VMEM((2, width, width), F32),
+            ],
             aliases={} if first else {at + one: one for one in range(4)},
             flops=6 * batch * peers * count * count * width,
             limit=16,
@@ -366,14 +367,20 @@
     grad_first, grad_second = sum_towers(*state, groups)
     sends = []
     halves = [range(groups // 2, groups), range(groups // 2)]
-    for steps in halves:
+    for half, steps in enumerate(halves):
         outs = call(
             functools.partial(compact_kernel, cap, peers, groups, steps),
             [dscore, vecs, *metas],
-            [jax.ShapeDtypeStruct((width // groups, peers * cap), BF16)] * len(steps),
+            [jax.ShapeDtypeStruct((width // groups, peers * cap), BF16)] * len(steps)
+            + [jax.ShapeDtypeStruct((1, peers * cap), F32)] * (half == 0),
             flops=pairs * pairs * width,
         )
+        if half == 0:
+            *outs, rows = outs
         sends = [*outs, *sends]
+    all_rows = [rows]
+    for step in range(1, groups):
+        all_rows.append(to_partner(rows, step, groups))
     got = [sends[0]]
     for step in range(1, groups):
         got.append(to_partner(sends[step], step, groups))

time: 72.2 us -> 71.3 us (0.988)
    pallas_call x10 -> x9, Pallas kernels: 23.5 us -> 23.1 us  [call(): pl.pallas_call(kernel, out_shape=shapes, in_specs=[VMEM] * len(args), out...]
  transfers between devices with their start and end apart: 23 -> 23, of which waited for: 8 -> 9; matrix products, arithmetic and copies ran while one was open for 1% -> 1% of each run, Pallas kernels for 29% -> 29%
where the time goes in v2:
time: 71.3 us; the launch traced here: 71.1 us
  starting transfers between devices  25.2 us (35%)
  Pallas kernels  24.6 us (35%)
  waiting for transfers between devices  18.8 us (26%)
  other arithmetic  1.6 us (2%)
  between operations  0.84 us (1%)
    pallas_call x9, Pallas kernels, call(): pl.pallas_call(kernel, out_shape=shapes, in_specs=[VMEM] * len(args), out...  23.1 us
    ppermute x14, starting transfers between devices, along(): lax.ppermute(value, 'rows', [(one, one ^ bit) for one in range(size)])  19 us
    ppermute x9, waiting for transfers between devices, to_partner(): return lax.ppermute(value, 'grp', pairs)  11.6 us
    ppermute x14, waiting for transfers between devices, along(): lax.ppermute(value, 'rows', [(one, one ^ bit) for one in range(size)])  7.28 us
    ppermute x9, starting transfers between devices, to_partner(): return lax.ppermute(value, 'grp', pairs)  6.18 us
    pallas_call x1, Pallas kernels, whole_group_step(): pl.pallas_call(pack_kernel, out_shape=jax.ShapeDtypeStruct((META, width),...  1.43 us
  transfers between devices with their start and end apart: 23, of which 9 were waited for; matrix products, arithmetic and copies ran while one was open for 1% of the time, Pallas kernels for 29%

profile of v2, /device:TPU:0, one launch (start us, length us, event | category | flops | bytes accessed | tf_op | source)
XLA Modules:
  0.0 71.1 jit_solution(1006924577846871901)
XLA Ops:
  0.6 4.1 %collective-permute-start.7 = (bf16[256,256]{1,0:T(8,128)(2,1)}, bf16[256,256]{1,0:T(8,128)(2,1)S(1)}, u32[]{:S(2)}, u32[]{:S(2)}) collective-permute-start(bf16[256,256]{1,0:T(8,128)(2,1)} %bitcast.4), channel_id=1, source_target_pairs={{0,16},{4,20},{8,24},{12,28},{16,0},{20,4},{24,8},{28,12},{1,17},{... | collective-permute-start | bytes 393224 | tf_op jit(solution)/shard_map/ppermute | solution.py:276
  4.8 1.4 %shard_map.103.refs_2_ = bf16[16,256]{1,0:T(8,128)(2,1)} custom-call(f32[1,256]{1,0:T(1,128)} %weight_hbm.1, s32[1,256]{1,0:T(1,128)} %target_hbm.1, s32[1,256]{1,0:T(1,128)} %bitcast.10, s32[1,256]{1,0:T(1,128)} %row_hbm.1), custom_call_target="tpu_custom_call" | custom-call | flops 8589934592 | bytes 1048576 | tf_op jit(solution)/shard_map/pallas_call | solution.py:316
  7.1 1.9 %collective-permute-start.5 = (bf16[256,256]{1,0:T(8,128)(2,1)S(1)}, bf16[256,256]{1,0:T(8,128)(2,1)S(1)}, u32[]{:S(2)}, u32[]{:S(2)}) collective-permute-start(bf16[256,256]{1,0:T(8,128)(2,1)S(1)} %bitcast.5), channel_id=1, source_target_pairs={{0,8},{4,12},{8,0},{12,4},{16,24},{20,28},{24,16},{28,20},{1,9},{5... | collective-permute-start | bytes 393224 | tf_op jit(solution)/shard_map/ppermute | solution.py:276
  8.9 1.5 %collective-permute-start.4 = (bf16[256,256]{1,0:T(8,128)(2,1)S(1)}, bf16[256,256]{1,0:T(8,128)(2,1)S(1)}, u32[]{:S(2)}, u32[]{:S(2)}) collective-permute-start(bf16[256,256]{1,0:T(8,128)(2,1)S(1)} %bitcast.6), channel_id=1, source_target_pairs={{0,4},{4,0},{8,12},{12,8},{16,20},{20,16},{24,28},{28,24},{1,5},{5... | collective-permute-start | bytes 393224 | tf_op jit(solution)/shard_map/ppermute | solution.py:276
  10.4 4.4 %collective-permute-done.7.refs_6_ = bf16[256,256]{1,0:T(8,128)(2,1)S(1)} collective-permute-done((bf16[256,256]{1,0:T(8,128)(2,1)}, bf16[256,256]{1,0:T(8,128)(2,1)S(1)}, u32[]{:S(2)}, u32[]{:S(2)}) %collective-permute-start.7) | collective-permute-done | bytes 131104 | tf_op jit(solution)/shard_map/ppermute | solution.py:276
  15.2 1.7 %collective-permute-start.3 = (bf16[272,256]{1,0:T(8,128)(2,1)S(1)}, bf16[272,256]{1,0:T(8,128)(2,1)S(1)}, u32[]{:S(2)}, u32[]{:S(2)}) collective-permute-start(bf16[272,256]{1,0:T(8,128)(2,1)S(1)} %pad_maximum_fusion.refs_0_), channel_id=1, source_target_pairs={{0,4},{4,0},{8,12},{12,8},{16,20},{20,16},{24,28},{28,24},{1,5},{5... | collective-permute-start | bytes 417800 | tf_op jit(solution)/shard_map/ppermute | solution.py:276
  17.4 1.6 %collective-permute-start.1 = (bf16[272,256]{1,0:T(8,128)(2,1)S(1)}, bf16[272,256]{1,0:T(8,128)(2,1)S(1)}, u32[]{:S(2)}, u32[]{:S(2)}) collective-permute-start(bf16[272,256]{1,0:T(8,128)(2,1)S(1)} %collective-permute-done.refs_0_), channel_id=1, source_target_pairs={{0,8},{4,12},{8,0},{12,4},{16,24},{20,28},{24,16},{28,20},{1,9},{5... | collective-permute-start | bytes 417800 | tf_op jit(solution)/shard_map/ppermute | solution.py:276
  19.5 1.5 %collective-permute-start.6 = (bf16[256,256]{1,0:T(8,128)(2,1)S(1)}, bf16[256,256]{1,0:T(8,128)(2,1)S(1)}, u32[]{:S(2)}, u32[]{:S(2)}) collective-permute-start(bf16[256,256]{1,0:T(8,128)(2,1)S(1)} %collective-permute-done.4.refs_3_), channel_id=1, source_target_pairs={{0,8},{4,12},{8,0},{12,4},{16,24},{20,28},{24,16},{28,20},{1,9},{5... | collective-permute-start | bytes 393224 | tf_op jit(solution)/shard_map/ppermute | solution.py:276
  21.1 2.3 %collective-permute-start.10 = (bf16[256,256]{1,0:T(8,128)(2,1)S(1)}, bf16[256,256]{1,0:T(8,128)(2,1)S(1)}, u32[]{:S(2)}, u32[]{:S(2)}) collective-permute-start(bf16[256,256]{1,0:T(8,128)(2,1)S(1)} %collective-permute-done.9.refs_8_), channel_id=1, source_target_pairs={{0,4},{4,0},{8,12},{12,8},{16,20},{20,16},{24,28},{28,24},{1,5},{5... | collective-permute-start | bytes 393224 | tf_op jit(solution)/shard_map/ppermute | solution.py:276
  23.3 1.3 %collective-permute-done.8.refs_7_ = bf16[256,256]{1,0:T(8,128)(2,1)S(1)} collective-permute-done((bf16[256,256]{1,0:T(8,128)(2,1)S(1)}, bf16[256,256]{1,0:T(8,128)(2,1)S(1)}, u32[]{:S(2)}, u32[]{:S(2)}) %collective-permute-start.8) | collective-permute-done | bytes 131104 | tf_op jit(solution)/shard_map/ppermute | solution.py:276
  26.9 1.5 %collective-permute-start.13 = (bf16[272,256]{1,0:T(8,128)(2,1)S(1)}, bf16[272,256]{1,0:T(8,128)(2,1)S(1)}, u32[]{:S(2)}, u32[]{:S(2)}) collective-permute-start(bf16[272,256]{1,0:T(8,128)(2,1)S(1)} %collective-permute-done.3.refs_1_), channel_id=1, source_target_pairs={{0,8},{4,12},{8,0},{12,4},{16,24},{20,28},{24,16},{28,20},{1,9},{5... | collective-permute-start | bytes 417800 | tf_op jit(solution)/shard_map/ppermute | solution.py:276
  29.1 3.7 %shard_map.104 = (bf16[2048,2048]{1,0:T(8,128)(2,1)S(1)}, bf16[256,2048]{1,0:T(8,128)(2,1)S(1)}, f32[256,256]{1,0:T(8,128)S(1)}, f32[256,256]{1,0:T(8,128)S(1)}, bf16[2048,256]{1,0:T(8,128)(2,1)S(1)}) custom-call(bf16[272,256]{1,0:T(8,128)(2,1)S(1)} %pad_maximum_fusion.refs_0_, bf16[272,256]{1,0:T(8,128)(2,1)S(1)} %collective-permute-done.3.refs_1_, ...), custom_call_target="tpu_custom_call" | custom-call | flops 1610612736 | bytes 1048576 | tf_op jit(solution)/shard_map/pallas_call | solution.py:249
  32.9 3.7 %shard_map.105 = (bf16[2048,2048]{1,0:T(8,128)(2,1)S(1)}, bf16[256,2048]{1,0:T(8,128)(2,1)S(1)}, f32[256,256]{1,0:T(8,128)S(1)}, f32[256,256]{1,0:T(8,128)S(1)}) custom-call(bf16[272,256]{1,0:T(8,128)(2,1)S(1)} %collective-permute-done.12.refs_0_, ...), custom_call_target="tpu_custom_call", output_to_operand_aliasing={{0}: (5, {}), {1}: (6, {}), {2}: (7, {}), {3}: (8, {})} | custom-call | flops 1610612736 | bytes 1048576 | tf_op jit(solution)/shard_map/pallas_call | solution.py:249
  36.6 3.7 %shard_map.106 = (bf16[2048,2048]{1,0:T(8,128)(2,1)S(1)}, bf16[256,2048]{1,0:T(8,128)(2,1)S(1)}, f32[256,256]{1,0:T(8,128)S(1)}, f32[256,256]{1,0:T(8,128)S(1)}) custom-call(bf16[272,256]{1,0:T(8,128)(2,1)S(1)} %collective-permute-done.refs_0_, ...), custom_call_target="tpu_custom_call", output_to_operand_aliasing={{0}: (5, {}), {1}: (6, {}), {2}: (7, {}), {3}: (8, {})} | custom-call | flops 1610612736 | bytes 1048576 | tf_op jit(solution)/shard_map/pallas_call | solution.py:249
  40.4 4.0 %shard_map.107 = (bf16[2048,2048]{1,0:T(8,128)(2,1)S(1)}, bf16[256,2048]{1,0:T(8,128)(2,1)S(1)}, f32[256,256]{1,0:T(8,128)S(1)}, f32[256,256]{1,0:T(8,128)S(1)}) custom-call(bf16[272,256]{1,0:T(8,128)(2,1)S(1)} %collective-permute-done.1.refs_0_, ...), custom_call_target="tpu_custom_call", output_to_operand_aliasing={{0}: (5, {}), {1}: (6, {}), {2}: (7, {}), {3}: (8, {})} | custom-call | flops 1610612736 | bytes 1048576 | tf_op jit(solution)/shard_map/pallas_call | solution.py:249
  44.4 1.5 %collective-permute-done.14 = f32[256,256]{1,0:T(8,128)S(1)} collective-permute-done((f32[256,256]{1,0:T(8,128)S(1)}, f32[256,256]{1,0:T(8,128)S(1)}, u32[]{:S(2)}, u32[]{:S(2)}) %collective-permute-start.14) | collective-permute-done | bytes 262176 | tf_op jit(solution)/shard_map/ppermute | solution.py:272
  46.0 1.6 %collective-permute-start.15 = (f32[256,256]{1,0:T(8,128)S(1)}, f32[256,256]{1,0:T(8,128)S(1)}, u32[]{:S(2)}, u32[]{:S(2)}) collective-permute-start(f32[256,256]{1,0:T(8,128)S(1)} %add.11), channel_id=1, source_target_pairs={{0,2},{1,3},{2,0},{3,1},{4,6},{5,7},{6,4},{7,5},{8,10},{9,11},{10,... | collective-permute-start | bytes 786440 | tf_op jit(solution)/shard_map/ppermute | solution.py:272
  47.6 6.8 %collective-permute-done.15 = f32[256,256]{1,0:T(8,128)S(1)} collective-permute-done((f32[256,256]{1,0:T(8,128)S(1)}, f32[256,256]{1,0:T(8,128)S(1)}, u32[]{:S(2)}, u32[]{:S(2)}) %collective-permute-start.15) | collective-permute-done | bytes 262176 | tf_op jit(solution)/shard_map/ppermute | solution.py:272
  54.5 2.0 %shard_map.109 = (bf16[64,1024]{1,0:T(8,128)(2,1)S(1)}, bf16[64,1024]{1,0:T(8,128)(2,1)S(1)}) custom-call(bf16[2048,2048]{1,0:T(8,128)(2,1)S(1)} %get-tuple-element.40.refs_0_, bf16[256,2048]{1,0:T(8,128)(2,1)S(1)} %get-tuple-element.41.refs_1_, bf16[16,256]{1,0:T(8,128)(2,1)S(1)} %copy-done.2, bf16[16,256]{1,0:T(8,128)(2,1)S(1)} %slice.28.refs_3_, ...), custom_call_target="tpu_custom_call" | custom-call | flops 1073741824 | bytes 1048576 | tf_op jit(solution)/shard_map/pallas_call | solution.py:249
  57.1 2.3 %shard_map.108 = (bf16[64,1024]{1,0:T(8,128)(2,1)S(1)}, bf16[64,1024]{1,0:T(8,128)(2,1)S(1)}, f32[1,1024]{1,0:T(1,128)S(1)}) custom-call(bf16[2048,2048]{1,0:T(8,128)(2,1)S(1)} %get-tuple-element.40.refs_0_, bf16[256,2048]{1,0:T(8,128)(2,1)S(1)} %get-tuple-element.41.refs_1_, bf16[16,256]{1,0:T(8,128)(2,1)S(1)} %copy-done.2, ...), custom_call_target="tpu_custom_call" | custom-call | flops 1073741824 | bytes 1048576 | tf_op jit(solution)/shard_map/pallas_call | solution.py:249
  59.3 1.6 %collective-permute-start.19 = (bf16[64,1024]{1,0:T(8,128)(2,1)S(1)}, bf16[64,1024]{1,0:T(8,128)(2,1)S(1)}, u32[]{:S(2)}, u32[]{:S(2)}) collective-permute-start(bf16[64,1024]{1,0:T(8,128)(2,1)S(1)} %get-tuple-element.44), channel_id=1, source_target_pairs={{0,2},{1,3},{2,0},{3,1},{4,6},{5,7},{6,4},{7,5},{8,10},{9,11},{10,... | collective-permute-start | bytes 393224 | tf_op jit(solution)/shard_map/ppermute | solution.py:272
  62.4 1.5 %collective-permute-start.20 = (f32[1,1024]{1,0:T(1,128)S(1)}, f32[1,1024]{1,0:T(1,128)S(1)}, u32[]{:S(2)}, u32[]{:S(2)}) collective-permute-start(f32[1,1024]{1,0:T(1,128)S(1)} %get-tuple-element.43.refs_2_), channel_id=1, source_target_pairs={{0,2},{1,3},{2,0},{3,1},{4,6},{5,7},{6,4},{7,5},{8,10},{9,11},{10,... | collective-permute-start | bytes 12296 | tf_op jit(solution)/shard_map/ppermute | solution.py:272
  65.4 2.4 %collective-permute-done.20.refs_1_ = f32[1,1024]{1,0:T(1,128)S(1)} collective-permute-done((f32[1,1024]{1,0:T(1,128)S(1)}, f32[1,1024]{1,0:T(1,128)S(1)}, u32[]{:S(2)}, u32[]{:S(2)}) %collective-permute-start.20) | collective-permute-done | bytes 4128 | tf_op jit(solution)/shard_map/ppermute | solution.py:272
  68.6 1.7 %shard_map.112 = f32[64,4096]{1,0:T(8,128)} custom-call(bf16[64,1024]{1,0:T(8,128)(2,1)S(1)} %collective-permute-done.17.refs_0_, f32[1,1024]{1,0:T(1,128)S(1)} %collective-permute-done.18.refs_1_, f32[64,4096]{1,0:T(8,128)S(1)} %shard_map.111.refs_2_), custom_call_target="tpu_custom_call" | custom-call | flops 1048576 | bytes 1048576 | tf_op jit(solution)/shard_map/pallas_call | solution.py:249
  (53 shorter events, 10.5 us)
Async XLA Ops:
  0.6 14.2 %collective-permute-start.7 = (bf16[256,256]{1,0:T(8,128)(2,1)}, bf16[256,256]{1,0:T(8,128)(2,1)S(1)}, u32[]{:S(2)}, u32[]{:S(2)}) collective-permute-start(bf16[256,256]{1,0:T(8,128)(2,1)} %bitcast.4), channel_id=1, source_target_pairs={{0,16},{4,20},{8,24},{12,28},{16,0},{20,4},{24,8},{28,12},{1,17},{... | collective-permute-start | bytes 393224 | tf_op jit(solution)/shard_map/ppermute | solution.py:276
  4.8 24.4 %copy-start.1 = (bf16[256,256]{1,0:T(8,128)(2,1)S(1)}, bf16[256,256]{1,0:T(8,128)(2,1)}, u32[]{:S(2)}) copy-start(bf16[256,256]{1,0:T(8,128)(2,1)} %refs_4_.5) | copy-start | bytes 393220
  6.9 10.5 %collective-permute-start = (bf16[272,256]{1,0:T(8,128)(2,1)S(1)}, bf16[272,256]{1,0:T(8,128)(2,1)S(1)}, u32[]{:S(2)}, u32[]{:S(2)}) collective-permute-start(bf16[272,256]{1,0:T(8,128)(2,1)S(1)} %pad_maximum_fusion.refs_0_), channel_id=1, source_target_pairs={{0,16},{4,20},{8,24},{12,28},{16,0},{20,4},{24,8},{28,12},{1,17},{... | collective-permute-start | bytes 417800 | tf_op jit(solution)/shard_map/ppermute | solution.py:276
  7.1 11.9 %collective-permute-start.5 = (bf16[256,256]{1,0:T(8,128)(2,1)S(1)}, bf16[256,256]{1,0:T(8,128)(2,1)S(1)}, u32[]{:S(2)}, u32[]{:S(2)}) collective-permute-start(bf16[256,256]{1,0:T(8,128)(2,1)S(1)} %bitcast.5), channel_id=1, source_target_pairs={{0,8},{4,12},{8,0},{12,4},{16,24},{20,28},{24,16},{28,20},{1,9},{5... | collective-permute-start | bytes 393224 | tf_op jit(solution)/shard_map/ppermute | solution.py:276
  8.9 10.6 %collective-permute-start.4 = (bf16[256,256]{1,0:T(8,128)(2,1)S(1)}, bf16[256,256]{1,0:T(8,128)(2,1)S(1)}, u32[]{:S(2)}, u32[]{:S(2)}) collective-permute-start(bf16[256,256]{1,0:T(8,128)(2,1)S(1)} %bitcast.6), channel_id=1, source_target_pairs={{0,4},{4,0},{8,12},{12,8},{16,20},{20,16},{24,28},{28,24},{1,5},{5... | collective-permute-start | bytes 393224 | tf_op jit(solution)/shard_map/ppermute | solution.py:276
  14.9 6.2 %collective-permute-start.9 = (bf16[256,256]{1,0:T(8,128)(2,1)S(1)}, bf16[256,256]{1,0:T(8,128)(2,1)S(1)}, u32[]{:S(2)}, u32[]{:S(2)}) collective-permute-start(bf16[256,256]{1,0:T(8,128)(2,1)S(1)} %collective-permute-done.7.refs_6_), channel_id=1, source_target_pairs={{0,8},{4,12},{8,0},{12,4},{16,24},{20,28},{24,16},{28,20},{1,9},{5... | collective-permute-start | bytes 393224 | tf_op jit(solution)/shard_map/ppermute | solution.py:276
  15.2 8.1 %collective-permute-start.3 = (bf16[272,256]{1,0:T(8,128)(2,1)S(1)}, bf16[272,256]{1,0:T(8,128)(2,1)S(1)}, u32[]{:S(2)}, u32[]{:S(2)}) collective-permute-start(bf16[272,256]{1,0:T(8,128)(2,1)S(1)} %pad_maximum_fusion.refs_0_), channel_id=1, source_target_pairs={{0,4},{4,0},{8,12},{12,8},{16,20},{20,16},{24,28},{28,24},{1,5},{5... | collective-permute-start | bytes 417800 | tf_op jit(solution)/shard_map/ppermute | solution.py:276
  17.4 11.0 %collective-permute-start.1 = (bf16[272,256]{1,0:T(8,128)(2,1)S(1)}, bf16[272,256]{1,0:T(8,128)(2,1)S(1)}, u32[]{:S(2)}, u32[]{:S(2)}) collective-permute-start(bf16[272,256]{1,0:T(8,128)(2,1)S(1)} %collective-permute-done.refs_0_), channel_id=1, source_target_pairs={{0,8},{4,12},{8,0},{12,4},{16,24},{20,28},{24,16},{28,20},{1,9},{5... | collective-permute-start | bytes 417800 | tf_op jit(solution)/shard_map/ppermute | solution.py:276
  19.0 5.7 %collective-permute-start.8 = (bf16[256,256]{1,0:T(8,128)(2,1)S(1)}, bf16[256,256]{1,0:T(8,128)(2,1)S(1)}, u32[]{:S(2)}, u32[]{:S(2)}) collective-permute-start(bf16[256,256]{1,0:T(8,128)(2,1)S(1)} %collective-permute-done.7.refs_6_), channel_id=1, source_target_pairs={{0,4},{4,0},{8,12},{12,8},{16,20},{20,16},{24,28},{28,24},{1,5},{5... | collective-permute-start | bytes 393224 | tf_op jit(solution)/shard_map/ppermute | solution.py:276
  19.5 7.3 %collective-permute-start.6 = (bf16[256,256]{1,0:T(8,128)(2,1)S(1)}, bf16[256,256]{1,0:T(8,128)(2,1)S(1)}, u32[]{:S(2)}, u32[]{:S(2)}) collective-permute-start(bf16[256,256]{1,0:T(8,128)(2,1)S(1)} %collective-permute-done.4.refs_3_), channel_id=1, source_target_pairs={{0,8},{4,12},{8,0},{12,4},{16,24},{20,28},{24,16},{28,20},{1,9},{5... | collective-permute-start | bytes 393224 | tf_op jit(solution)/shard_map/ppermute | solution.py:276
  21.1 8.1 %collective-permute-start.10 = (bf16[256,256]{1,0:T(8,128)(2,1)S(1)}, bf16[256,256]{1,0:T(8,128)(2,1)S(1)}, u32[]{:S(2)}, u32[]{:S(2)}) collective-permute-start(bf16[256,256]{1,0:T(8,128)(2,1)S(1)} %collective-permute-done.9.refs_8_), channel_id=1, source_target_pairs={{0,4},{4,0},{8,12},{12,8},{16,20},{20,16},{24,28},{28,24},{1,5},{5... | collective-permute-start | bytes 393224 | tf_op jit(solution)/shard_map/ppermute | solution.py:276
  23.3 9.5 %collective-permute-start.12 = (bf16[272,256]{1,0:T(8,128)(2,1)S(1)}, bf16[272,256]{1,0:T(8,128)(2,1)S(1)}, u32[]{:S(2)}, u32[]{:S(2)}) collective-permute-start(bf16[272,256]{1,0:T(8,128)(2,1)S(1)} %pad_maximum_fusion.refs_0_), channel_id=1, source_target_pairs={{0,8},{4,12},{8,0},{12,4},{16,24},{20,28},{24,16},{28,20},{1,9},{5... | collective-permute-start | bytes 417800 | tf_op jit(solution)/shard_map/ppermute | solution.py:276
  24.7 11.9 %collective-permute-start.11 = (bf16[272,256]{1,0:T(8,128)(2,1)S(1)}, bf16[272,256]{1,0:T(8,128)(2,1)S(1)}, u32[]{:S(2)}, u32[]{:S(2)}) collective-permute-start(bf16[272,256]{1,0:T(8,128)(2,1)S(1)} %collective-permute-done.refs_0_), channel_id=1, source_target_pairs={{0,4},{4,0},{8,12},{12,8},{16,20},{20,16},{24,28},{28,24},{1,5},{5... | collective-permute-start | bytes 417800 | tf_op jit(solution)/shard_map/ppermute | solution.py:276
  26.9 6.0 %collective-permute-start.13 = (bf16[272,256]{1,0:T(8,128)(2,1)S(1)}, bf16[272,256]{1,0:T(8,128)(2,1)S(1)}, u32[]{:S(2)}, u32[]{:S(2)}) collective-permute-start(bf16[272,256]{1,0:T(8,128)(2,1)S(1)} %collective-permute-done.3.refs_1_), channel_id=1, source_target_pairs={{0,8},{4,12},{8,0},{12,4},{16,24},{20,28},{24,16},{28,20},{1,9},{5... | collective-permute-start | bytes 417800 | tf_op jit(solution)/shard_map/ppermute | solution.py:276
  28.3 12.0 %collective-permute-start.2 = (bf16[272,256]{1,0:T(8,128)(2,1)S(1)}, bf16[272,256]{1,0:T(8,128)(2,1)S(1)}, u32[]{:S(2)}, u32[]{:S(2)}) collective-permute-start(bf16[272,256]{1,0:T(8,128)(2,1)S(1)} %collective-permute-done.1.refs_0_), channel_id=1, source_target_pairs={{0,4},{4,0},{8,12},{12,8},{16,20},{20,16},{24,28},{28,24},{1,5},{5... | collective-permute-start | bytes 417800 | tf_op jit(solution)/shard_map/ppermute | solution.py:276
  44.4 1.6 %collective-permute-start.14 = (f32[256,256]{1,0:T(8,128)S(1)}, f32[256,256]{1,0:T(8,128)S(1)}, u32[]{:S(2)}, u32[]{:S(2)}) collective-permute-start(f32[256,256]{1,0:T(8,128)S(1)} %get-tuple-element.39), channel_id=1, source_target_pairs={{0,1},{1,0},{2,3},{3,2},{4,5},{5,4},{6,7},{7,6},{8,9},{9,8},{10,11... | collective-permute-start | bytes 786440 | tf_op jit(solution)/shard_map/ppermute | solution.py:272
  46.0 8.4 %collective-permute-start.15 = (f32[256,256]{1,0:T(8,128)S(1)}, f32[256,256]{1,0:T(8,128)S(1)}, u32[]{:S(2)}, u32[]{:S(2)}) collective-permute-start(f32[256,256]{1,0:T(8,128)S(1)} %add.11), channel_id=1, source_target_pairs={{0,2},{1,3},{2,0},{3,1},{4,6},{5,7},{6,4},{7,5},{8,10},{9,11},{10,... | collective-permute-start | bytes 786440 | tf_op jit(solution)/shard_map/ppermute | solution.py:272
  54.5 15.8 %collective-permute-start.16 = (f32[256,256]{1,0:T(8,128)S(1)}, f32[256,256]{1,0:T(8,128)S(1)}, u32[]{:S(2)}, u32[]{:S(2)}) collective-permute-start(f32[256,256]{1,0:T(8,128)S(1)} %add.12), channel_id=1, source_target_pairs={{0,1},{1,0},{2,3},{3,2},{4,5},{5,4},{6,7},{7,6},{8,9},{9,8},{10,11... | collective-permute-start | bytes 786440 | tf_op jit(solution)/shard_map/ppermute | solution.py:272
  56.5 7.4 %collective-permute-start.21 = (bf16[64,1024]{1,0:T(8,128)(2,1)S(1)}, bf16[64,1024]{1,0:T(8,128)(2,1)S(1)}, u32[]{:S(2)}, u32[]{:S(2)}) collective-permute-start(bf16[64,1024]{1,0:T(8,128)(2,1)S(1)} %get-tuple-element.46), channel_id=1, source_target_pairs={{0,1},{1,0},{2,3},{3,2},{4,5},{5,4},{6,7},{7,6},{8,9},{9,8},{10,11... | collective-permute-start | bytes 393224 | tf_op jit(solution)/shard_map/ppermute | solution.py:272
  59.3 8.4 %collective-permute-start.19 = (bf16[64,1024]{1,0:T(8,128)(2,1)S(1)}, bf16[64,1024]{1,0:T(8,128)(2,1)S(1)}, u32[]{:S(2)}, u32[]{:S(2)}) collective-permute-start(bf16[64,1024]{1,0:T(8,128)(2,1)S(1)} %get-tuple-element.44), channel_id=1, source_target_pairs={{0,2},{1,3},{2,0},{3,1},{4,6},{5,7},{6,4},{7,5},{8,10},{9,11},{10,... | collective-permute-start | bytes 393224 | tf_op jit(solution)/shard_map/ppermute | solution.py:272
  60.9 7.6 %collective-permute-start.17 = (bf16[64,1024]{1,0:T(8,128)(2,1)S(1)}, bf16[64,1024]{1,0:T(8,128)(2,1)S(1)}, u32[]{:S(2)}, u32[]{:S(2)}) collective-permute-start(bf16[64,1024]{1,0:T(8,128)(2,1)S(1)} %get-tuple-element.42), channel_id=1, source_target_pairs={{0,3},{1,2},{2,1},{3,0},{4,7},{5,6},{6,5},{7,4},{8,11},{9,10},{10,... | collective-permute-start | bytes 393224 | tf_op jit(solution)/shard_map/ppermute | solution.py:272
  60.9 1.4 %collective-permute-start.22 = (f32[1,1024]{1,0:T(1,128)S(1)}, f32[1,1024]{1,0:T(1,128)S(1)}, u32[]{:S(2)}, u32[]{:S(2)}) collective-permute-start(f32[1,1024]{1,0:T(1,128)S(1)} %get-tuple-element.43.refs_2_), channel_id=1, source_target_pairs={{0,1},{1,0},{2,3},{3,2},{4,5},{5,4},{6,7},{7,6},{8,9},{9,8},{10,11... | collective-permute-start | bytes 12296 | tf_op jit(solution)/shard_map/ppermute | solution.py:272
  62.4 5.4 %collective-permute-start.20 = (f32[1,1024]{1,0:T(1,128)S(1)}, f32[1,1024]{1,0:T(1,128)S(1)}, u32[]{:S(2)}, u32[]{:S(2)}) collective-permute-start(f32[1,1024]{1,0:T(1,128)S(1)} %get-tuple-element.43.refs_2_), channel_id=1, source_target_pairs={{0,2},{1,3},{2,0},{3,1},{4,6},{5,7},{6,4},{7,5},{8,10},{9,11},{10,... | collective-permute-start | bytes 12296 | tf_op jit(solution)/shard_map/ppermute | solution.py:272
  63.9 4.7 %collective-permute-start.18 = (f32[1,1024]{1,0:T(1,128)S(1)}, f32[1,1024]{1,0:T(1,128)S(1)}, u32[]{:S(2)}, u32[]{:S(2)}) collective-permute-start(f32[1,1024]{1,0:T(1,128)S(1)} %get-tuple-element.43.refs_2_), channel_id=1, source_target_pairs={{0,3},{1,2},{2,1},{3,0},{4,7},{5,6},{6,5},{7,4},{8,11},{9,10},{10,... | collective-permute-start | bytes 12296 | tf_op jit(solution)/shard_map/ppermute | solution.py:272
  (4 other events, 42.3 us)

commit v3 on v2

--- a/solution.py
+++ b/solution.py
@@ -74,7 +74,7 @@
     refs = refs[4:]
     if first:
         items_ref, refs = refs[0], refs[1:]
-    scores_ref, slopes_ref, hidden_ref, sums_ref = refs
+    scores_ref, slopes_ref, hidden_ref, sums_ref, weight_ref, target_ref, held_ref, grad_ref = refs
     count = user_refs[0].shape[0] - META
     lanes = 128
     tall = 16
@@ -85,39 +85,41 @@
             items_ref[slot * count : (slot + 1) * count, :] = item_refs[slot][...]
     w_first = first_ref[...]
     w_second = second_ref[...]
-    lane = lax.broadcasted_iota(jnp.int32, (tall, lanes), 1)
     lines = count // tall
-    stride = max(1, lines // slots)
 
     def span(slot):
         return slice(slot * count, (slot + 1) * count)
 
-    state = [None] * users
+    wide = 4
+    turns = lines // wide
+    chunk = slots * count // turns
 
     def enter(user):
         features = user_refs[user][0:count, :]
         meta = jnp.transpose(user_refs[user][count : count + META, :].astype(F32))
         weight = meta[:, 5:6] + meta[:, 6:7] + meta[:, 7:8]
         target = (meta[:, 3:4] * 256.0 + meta[:, 4:5]).astype(jnp.int32)
+        weight_ref[user] = jnp.broadcast_to(weight, (count, lanes))
+        target_ref[user] = lax.broadcasted_iota(jnp.int32, (count, lanes), 1) - target
         pre_act = dot_nn(features, w_first)
         gate = jax.nn.sigmoid(pre_act)
         hidden = (pre_act * gate).astype(BF16)
-        slopes_ref[user % 3] = gate * (1.0 + pre_act * (1.0 - gate))
-        hidden_ref[user % 3] = hidden
+        slopes_ref[user] = gate * (1.0 + pre_act * (1.0 - gate))
+        hidden_ref[user] = hidden
         vecs = dot_nn(hidden, w_second).astype(BF16)
         vecs_ref[:, span(begin + user)] = jnp.transpose(vecs)
-        state[user] = [weight, target, vecs, None]
-
-    def score(user, slot):
-        part = contract_last(state[user][2], items_ref[span(slot), :])
-        scores_ref[user % 2, :, span(slot)] = part
+        held_ref[user] = vecs
+
+    def score(user, turn):
+        spot = pl.ds(turn * chunk, chunk)
+        scores_ref[user, :, spot] = contract_last(held_ref[user], items_ref[spot, :])
 
     def soften(user, line):
-        rows = slice(line * tall, (line + 1) * tall)
-        weight = state[user][0][rows]
-        away = lane - state[user][1][rows]
+        rows = pl.ds(line * tall, tall)
+        weight = weight_ref[user, rows, :]
+        away = target_ref[user, rows, :]
         total_lanes = slots * count
-        parts = [scores_ref[user % 2, rows, at : at + lanes] for at in range(0, total_lanes, lanes)]
+        parts = [scores_ref[user, rows, at : at + lanes] for at in range(0, total_lanes, lanes)]
         top = parts[0]
         for part in parts[1:]:
             top = jnp.maximum(top, part)
@@ -132,23 +134,19 @@
             base = (me ^ (start // count)) * count + start % count
             part = part * scale
             part = jnp.where(away == -base, part - weight, part)
-            out = slice((begin + user) * count + line * tall, (begin + user) * count + (line + 1) * tall)
+            out = pl.ds((begin + user) * count + line * tall, tall)
             dscore_ref[out, start : start + lanes] = part.astype(BF16)
 
-    def pull(user, piece):
-        one = state[user]
-        rows = span(begin + user)
-        half = slots * count // 2
-        if piece == 0:
-            one[3] = dot_nn(dscore_ref[rows, :half], items_ref[:half, :])
-        elif piece == 1:
-            one[3] = (one[3] + dot_nn(dscore_ref[rows, half:], items_ref[half:, :])).astype(BF16)
-        elif piece == 2:
-            keep(second_sum, 1, user, contract_first(hidden_ref[user % 3], one[3]))
-            one[3] = contract_last(one[3], w_second)
-        else:
-            grad_pre = (one[3] * slopes_ref[user % 3]).astype(BF16)
-            keep(first_sum, 0, user, contract_first(user_refs[user][0:count, :], grad_pre))
+    def gather_grad(user, turn):
+        spot = pl.ds(turn * chunk, chunk)
+        term = dot_nn(dscore_ref[span(begin + user), spot], items_ref[spot, :])
+        grad_ref[user] = grad_ref[user] + term
+
+    def pull(user):
+        grad_user = grad_ref[user].astype(BF16)
+        keep(second_sum, 1, user, contract_first(hidden_ref[user], grad_user))
+        grad_pre = (contract_last(grad_user, w_second) * slopes_ref[user]).astype(BF16)
+        keep(first_sum, 0, user, contract_first(user_refs[user][0:count, :], grad_pre))
 
     def keep(ref, index, user, value):
         if user:
@@ -157,16 +155,28 @@
             ref[...] = value if first else (mine_in, other_in)[index][...] + value
 
     first_sum, second_sum = (mine_ref, other_ref) if not last else (sums_ref.at[0], sums_ref.at[1])
-    for step in range(users + 2):
-        if step < users:
-            enter(step)
-        for line in range(lines):
-            if step < users and line % stride == 0 and line // stride < slots:
-                score(step, line // stride)
-            if 1 <= step <= users:
-                soften(step - 1, line)
-            if 2 <= step and line % (lines // 4) == 0:
-                pull(step - 2, line // (lines // 4))
+    for user in range(users):
+        enter(user)
+        grad_ref[user] = jnp.zeros_like(grad_ref[user])
+    for turn in range(turns):
+        score(0, turn)
+    for user in range(users):
+
+        def body(turn, carry):
+            if user + 1 < users:
+                score(user + 1, turn)
+            if user:
+                gather_grad(user - 1, turn)
+            for line in range(wide):
+                soften(user, turn * wide + line)
+            return carry
+
+        for turn in range(turns):
+            body(turn, 0)
+    for turn in range(turns):
+        gather_grad(users - 1, turn)
+    for user in range(users):
+        pull(user)
     if last:
         mine_ref[...] = jnp.where(flip, sums_ref[1], sums_ref[0])
         other_ref[...] = jnp.where(flip, sums_ref[0], sums_ref[1])
@@ -352,10 +362,14 @@
             args,
             shapes,
             scratch=[
-                pltpu.VMEM((2, count, pairs), F32),
-                pltpu.VMEM((3, count, width), F32),
-                pltpu.VMEM((3, count, width), BF16),
+                pltpu.VMEM((batch, count, pairs), F32),
+                pltpu.VMEM((batch, count, width), F32),
+                pltpu.VMEM((batch, count, width), BF16),
                 pltpu.VMEM((2, width, width), F32),
+                pltpu.VMEM((batch, count, 128), F32),
+                pltpu.VMEM((batch, count, 128), jnp.int32),
+                pltpu.VMEM((batch, count, width), BF16),
+                pltpu.VMEM((batch, count, width), F32),
             ],
             aliases={} if first else {at + one: one for one in range(4)},
             flops=6 * batch * peers * count * count * width,

time: 71.3 us -> 69.3 us (0.972)
  Pallas kernels: 24.6 us -> 22.5 us
    pallas_call x9, Pallas kernels: 23.1 us -> 21.1 us  [call(): pl.pallas_call(kernel, out_shape=shapes, in_specs=[VMEM] * len(args), out...]
  transfers between devices with their start and end apart: 23 -> 23, of which waited for: 9 -> 9; matrix products, arithmetic and copies ran while one was open for 1% -> 1% of each run, Pallas kernels for 29% -> 28%
where the time goes in v3:
time: 69.3 us; the launch traced here: 69.1 us
  starting transfers between devices  25.6 us (37%)
  Pallas kernels  22.5 us (32%)
  waiting for transfers between devices  18.6 us (27%)
  other arithmetic  1.6 us (2%)
  between operations  0.84 us (1%)
    pallas_call x9, Pallas kernels, call(): pl.pallas_call(kernel, out_shape=shapes, in_specs=[VMEM] * len(args), out...  21.1 us
    ppermute x14, starting transfers between devices, along(): lax.ppermute(value, 'rows', [(one, one ^ bit) for one in range(size)])  19 us
    ppermute x9, waiting for transfers between devices, to_partner(): return lax.ppermute(value, 'grp', pairs)  11.3 us
    ppermute x14, waiting for transfers between devices, along(): lax.ppermute(value, 'rows', [(one, one ^ bit) for one in range(size)])  7.28 us
    ppermute x9, starting transfers between devices, to_partner(): return lax.ppermute(value, 'grp', pairs)  6.53 us
    pallas_call x1, Pallas kernels, whole_group_step(): pl.pallas_call(pack_kernel, out_shape=jax.ShapeDtypeStruct((META, width),...  1.43 us
  transfers between devices with their start and end apart: 23, of which 9 were waited for; matrix products, arithmetic and copies ran while one was open for 1% of the time, Pallas kernels for 28%

profile of v3, /device:TPU:0, one launch (start us, length us, event | category | flops | bytes accessed | tf_op | source)
XLA Modules:
  0.0 69.1 jit_solution(14900891152673498213)
XLA Ops:
  0.6 4.1 %collective-permute-start.7 = (bf16[256,256]{1,0:T(8,128)(2,1)}, bf16[256,256]{1,0:T(8,128)(2,1)S(1)}, u32[]{:S(2)}, u32[]{:S(2)}) collective-permute-start(bf16[256,256]{1,0:T(8,128)(2,1)} %bitcast.4), channel_id=1, source_target_pairs={{0,16},{4,20},{8,24},{12,28},{16,0},{20,4},{24,8},{28,12},{1,17},{... | collective-permute-start | bytes 393224 | tf_op jit(solution)/shard_map/ppermute | solution.py:286
  4.8 1.4 %shard_map.103.refs_2_ = bf16[16,256]{1,0:T(8,128)(2,1)} custom-call(f32[1,256]{1,0:T(1,128)} %weight_hbm.1, s32[1,256]{1,0:T(1,128)} %target_hbm.1, s32[1,256]{1,0:T(1,128)} %bitcast.10, s32[1,256]{1,0:T(1,128)} %row_hbm.1), custom_call_target="tpu_custom_call" | custom-call | flops 8589934592 | bytes 1048576 | tf_op jit(solution)/shard_map/pallas_call | solution.py:326
  7.1 1.9 %collective-permute-start.5 = (bf16[256,256]{1,0:T(8,128)(2,1)S(1)}, bf16[256,256]{1,0:T(8,128)(2,1)S(1)}, u32[]{:S(2)}, u32[]{:S(2)}) collective-permute-start(bf16[256,256]{1,0:T(8,128)(2,1)S(1)} %bitcast.5), channel_id=1, source_target_pairs={{0,8},{4,12},{8,0},{12,4},{16,24},{20,28},{24,16},{28,20},{1,9},{5... | collective-permute-start | bytes 393224 | tf_op jit(solution)/shard_map/ppermute | solution.py:286
  8.9 1.5 %collective-permute-start.4 = (bf16[256,256]{1,0:T(8,128)(2,1)S(1)}, bf16[256,256]{1,0:T(8,128)(2,1)S(1)}, u32[]{:S(2)}, u32[]{:S(2)}) collective-permute-start(bf16[256,256]{1,0:T(8,128)(2,1)S(1)} %bitcast.6), channel_id=1, source_target_pairs={{0,4},{4,0},{8,12},{12,8},{16,20},{20,16},{24,28},{28,24},{1,5},{5... | collective-permute-start | bytes 393224 | tf_op jit(solution)/shard_map/ppermute | solution.py:286
  10.4 4.4 %collective-permute-done.7.refs_6_ = bf16[256,256]{1,0:T(8,128)(2,1)S(1)} collective-permute-done((bf16[256,256]{1,0:T(8,128)(2,1)}, bf16[256,256]{1,0:T(8,128)(2,1)S(1)}, u32[]{:S(2)}, u32[]{:S(2)}) %collective-permute-start.7) | collective-permute-done | bytes 131104 | tf_op jit(solution)/shard_map/ppermute | solution.py:286
  15.2 1.7 %collective-permute-start.3 = (bf16[272,256]{1,0:T(8,128)(2,1)S(1)}, bf16[272,256]{1,0:T(8,128)(2,1)S(1)}, u32[]{:S(2)}, u32[]{:S(2)}) collective-permute-start(bf16[272,256]{1,0:T(8,128)(2,1)S(1)} %pad_maximum_fusion.refs_0_), channel_id=1, source_target_pairs={{0,4},{4,0},{8,12},{12,8},{16,20},{20,16},{24,28},{28,24},{1,5},{5... | collective-permute-start | bytes 417800 | tf_op jit(solution)/shard_map/ppermute | solution.py:286
  17.4 1.6 %collective-permute-start.1 = (bf16[272,256]{1,0:T(8,128)(2,1)S(1)}, bf16[272,256]{1,0:T(8,128)(2,1)S(1)}, u32[]{:S(2)}, u32[]{:S(2)}) collective-permute-start(bf16[272,256]{1,0:T(8,128)(2,1)S(1)} %collective-permute-done.refs_0_), channel_id=1, source_target_pairs={{0,8},{4,12},{8,0},{12,4},{16,24},{20,28},{24,16},{28,20},{1,9},{5... | collective-permute-start | bytes 417800 | tf_op jit(solution)/shard_map/ppermute | solution.py:286
  19.5 1.5 %collective-permute-start.6 = (bf16[256,256]{1,0:T(8,128)(2,1)S(1)}, bf16[256,256]{1,0:T(8,128)(2,1)S(1)}, u32[]{:S(2)}, u32[]{:S(2)}) collective-permute-start(bf16[256,256]{1,0:T(8,128)(2,1)S(1)} %collective-permute-done.4.refs_3_), channel_id=1, source_target_pairs={{0,8},{4,12},{8,0},{12,4},{16,24},{20,28},{24,16},{28,20},{1,9},{5... | collective-permute-start | bytes 393224 | tf_op jit(solution)/shard_map/ppermute | solution.py:286
  21.1 2.3 %collective-permute-start.10 = (bf16[256,256]{1,0:T(8,128)(2,1)S(1)}, bf16[256,256]{1,0:T(8,128)(2,1)S(1)}, u32[]{:S(2)}, u32[]{:S(2)}) collective-permute-start(bf16[256,256]{1,0:T(8,128)(2,1)S(1)} %collective-permute-done.9.refs_8_), channel_id=1, source_target_pairs={{0,4},{4,0},{8,12},{12,8},{16,20},{20,16},{24,28},{28,24},{1,5},{5... | collective-permute-start | bytes 393224 | tf_op jit(solution)/shard_map/ppermute | solution.py:286
  23.3 1.3 %collective-permute-done.8.refs_7_ = bf16[256,256]{1,0:T(8,128)(2,1)S(1)} collective-permute-done((bf16[256,256]{1,0:T(8,128)(2,1)S(1)}, bf16[256,256]{1,0:T(8,128)(2,1)S(1)}, u32[]{:S(2)}, u32[]{:S(2)}) %collective-permute-start.8) | collective-permute-done | bytes 131104 | tf_op jit(solution)/shard_map/ppermute | solution.py:286
  26.9 1.5 %collective-permute-start.13 = (bf16[272,256]{1,0:T(8,128)(2,1)S(1)}, bf16[272,256]{1,0:T(8,128)(2,1)S(1)}, u32[]{:S(2)}, u32[]{:S(2)}) collective-permute-start(bf16[272,256]{1,0:T(8,128)(2,1)S(1)} %collective-permute-done.3.refs_1_), channel_id=1, source_target_pairs={{0,8},{4,12},{8,0},{12,4},{16,24},{20,28},{24,16},{28,20},{1,9},{5... | collective-permute-start | bytes 417800 | tf_op jit(solution)/shard_map/ppermute | solution.py:286
  29.1 3.2 %shard_map.104 = (bf16[2048,2048]{1,0:T(8,128)(2,1)S(1)}, bf16[256,2048]{1,0:T(8,128)(2,1)S(1)}, f32[256,256]{1,0:T(8,128)S(1)}, f32[256,256]{1,0:T(8,128)S(1)}, bf16[2048,256]{1,0:T(8,128)(2,1)S(1)}) custom-call(bf16[272,256]{1,0:T(8,128)(2,1)S(1)} %pad_maximum_fusion.refs_0_, bf16[272,256]{1,0:T(8,128)(2,1)S(1)} %collective-permute-done.3.refs_1_, ...), custom_call_target="tpu_custom_call" | custom-call | flops 1610612736 | bytes 1048576 | tf_op jit(solution)/shard_map/pallas_call | solution.py:259
  32.4 3.2 %shard_map.105 = (bf16[2048,2048]{1,0:T(8,128)(2,1)S(1)}, bf16[256,2048]{1,0:T(8,128)(2,1)S(1)}, f32[256,256]{1,0:T(8,128)S(1)}, f32[256,256]{1,0:T(8,128)S(1)}) custom-call(bf16[272,256]{1,0:T(8,128)(2,1)S(1)} %collective-permute-done.12.refs_0_, ...), custom_call_target="tpu_custom_call", output_to_operand_aliasing={{0}: (5, {}), {1}: (6, {}), {2}: (7, {}), {3}: (8, {})} | custom-call | flops 1610612736 | bytes 1048576 | tf_op jit(solution)/shard_map/pallas_call | solution.py:259
  35.6 3.2 %shard_map.106 = (bf16[2048,2048]{1,0:T(8,128)(2,1)S(1)}, bf16[256,2048]{1,0:T(8,128)(2,1)S(1)}, f32[256,256]{1,0:T(8,128)S(1)}, f32[256,256]{1,0:T(8,128)S(1)}) custom-call(bf16[272,256]{1,0:T(8,128)(2,1)S(1)} %collective-permute-done.refs_0_, ...), custom_call_target="tpu_custom_call", output_to_operand_aliasing={{0}: (5, {}), {1}: (6, {}), {2}: (7, {}), {3}: (8, {})} | custom-call | flops 1610612736 | bytes 1048576 | tf_op jit(solution)/shard_map/pallas_call | solution.py:259
  38.8 3.4 %shard_map.107 = (bf16[2048,2048]{1,0:T(8,128)(2,1)S(1)}, bf16[256,2048]{1,0:T(8,128)(2,1)S(1)}, f32[256,256]{1,0:T(8,128)S(1)}, f32[256,256]{1,0:T(8,128)S(1)}) custom-call(bf16[272,256]{1,0:T(8,128)(2,1)S(1)} %collective-permute-done.1.refs_0_, ...), custom_call_target="tpu_custom_call", output_to_operand_aliasing={{0}: (5, {}), {1}: (6, {}), {2}: (7, {}), {3}: (8, {})} | custom-call | flops 1610612736 | bytes 1048576 | tf_op jit(solution)/shard_map/pallas_call | solution.py:259
  42.4 1.5 %collective-permute-done.14 = f32[256,256]{1,0:T(8,128)S(1)} collective-permute-done((f32[256,256]{1,0:T(8,128)S(1)}, f32[256,256]{1,0:T(8,128)S(1)}, u32[]{:S(2)}, u32[]{:S(2)}) %collective-permute-start.14) | collective-permute-done | bytes 262176 | tf_op jit(solution)/shard_map/ppermute | solution.py:282
  43.9 1.9 %collective-permute-start.15 = (f32[256,256]{1,0:T(8,128)S(1)}, f32[256,256]{1,0:T(8,128)S(1)}, u32[]{:S(2)}, u32[]{:S(2)}) collective-permute-start(f32[256,256]{1,0:T(8,128)S(1)} %add.11), channel_id=1, source_target_pairs={{0,2},{1,3},{2,0},{3,1},{4,6},{5,7},{6,4},{7,5},{8,10},{9,11},{10,... | collective-permute-start | bytes 786440 | tf_op jit(solution)/shard_map/ppermute | solution.py:282
  45.9 6.6 %collective-permute-done.15 = f32[256,256]{1,0:T(8,128)S(1)} collective-permute-done((f32[256,256]{1,0:T(8,128)S(1)}, f32[256,256]{1,0:T(8,128)S(1)}, u32[]{:S(2)}, u32[]{:S(2)}) %collective-permute-start.15) | collective-permute-done | bytes 262176 | tf_op jit(solution)/shard_map/ppermute | solution.py:282
  52.5 2.0 %shard_map.109 = (bf16[64,1024]{1,0:T(8,128)(2,1)S(1)}, bf16[64,1024]{1,0:T(8,128)(2,1)S(1)}) custom-call(bf16[2048,2048]{1,0:T(8,128)(2,1)S(1)} %get-tuple-element.40.refs_0_, bf16[256,2048]{1,0:T(8,128)(2,1)S(1)} %get-tuple-element.41.refs_1_, bf16[16,256]{1,0:T(8,128)(2,1)S(1)} %copy-done.2, bf16[16,256]{1,0:T(8,128)(2,1)S(1)} %slice.28.refs_3_, ...), custom_call_target="tpu_custom_call" | custom-call | flops 1073741824 | bytes 1048576 | tf_op jit(solution)/shard_map/pallas_call | solution.py:259
  55.1 2.3 %shard_map.108 = (bf16[64,1024]{1,0:T(8,128)(2,1)S(1)}, bf16[64,1024]{1,0:T(8,128)(2,1)S(1)}, f32[1,1024]{1,0:T(1,128)S(1)}) custom-call(bf16[2048,2048]{1,0:T(8,128)(2,1)S(1)} %get-tuple-element.40.refs_0_, bf16[256,2048]{1,0:T(8,128)(2,1)S(1)} %get-tuple-element.41.refs_1_, bf16[16,256]{1,0:T(8,128)(2,1)S(1)} %copy-done.2, ...), custom_call_target="tpu_custom_call" | custom-call | flops 1073741824 | bytes 1048576 | tf_op jit(solution)/shard_map/pallas_call | solution.py:259
  57.4 1.8 %collective-permute-start.19 = (bf16[64,1024]{1,0:T(8,128)(2,1)S(1)}, bf16[64,1024]{1,0:T(8,128)(2,1)S(1)}, u32[]{:S(2)}, u32[]{:S(2)}) collective-permute-start(bf16[64,1024]{1,0:T(8,128)(2,1)S(1)} %get-tuple-element.44), channel_id=1, source_target_pairs={{0,2},{1,3},{2,0},{3,1},{4,6},{5,7},{6,4},{7,5},{8,10},{9,11},{10,... | collective-permute-start | bytes 393224 | tf_op jit(solution)/shard_map/ppermute | solution.py:282
  60.4 1.7 %collective-permute-start.20 = (f32[1,1024]{1,0:T(1,128)S(1)}, f32[1,1024]{1,0:T(1,128)S(1)}, u32[]{:S(2)}, u32[]{:S(2)}) collective-permute-start(f32[1,1024]{1,0:T(1,128)S(1)} %get-tuple-element.43.refs_2_), channel_id=1, source_target_pairs={{0,2},{1,3},{2,0},{3,1},{4,6},{5,7},{6,4},{7,5},{8,10},{9,11},{10,... | collective-permute-start | bytes 12296 | tf_op jit(solution)/shard_map/ppermute | solution.py:282
  63.4 2.4 %collective-permute-done.20.refs_1_ = f32[1,1024]{1,0:T(1,128)S(1)} collective-permute-done((f32[1,1024]{1,0:T(1,128)S(1)}, f32[1,1024]{1,0:T(1,128)S(1)}, u32[]{:S(2)}, u32[]{:S(2)}) %collective-permute-start.20) | collective-permute-done | bytes 4128 | tf_op jit(solution)/shard_map/ppermute | solution.py:282
  66.6 1.7 %shard_map.112 = f32[64,4096]{1,0:T(8,128)} custom-call(bf16[64,1024]{1,0:T(8,128)(2,1)S(1)} %collective-permute-done.17.refs_0_, f32[1,1024]{1,0:T(1,128)S(1)} %collective-permute-done.18.refs_1_, f32[64,4096]{1,0:T(8,128)S(1)} %shard_map.111.refs_2_), custom_call_target="tpu_custom_call" | custom-call | flops 1048576 | bytes 1048576 | tf_op jit(solution)/shard_map/pallas_call | solution.py:259
  (53 shorter events, 10.1 us)
Async XLA Ops:
  0.6 14.2 %collective-permute-start.7 = (bf16[256,256]{1,0:T(8,128)(2,1)}, bf16[256,256]{1,0:T(8,128)(2,1)S(1)}, u32[]{:S(2)}, u32[]{:S(2)}) collective-permute-start(bf16[256,256]{1,0:T(8,128)(2,1)} %bitcast.4), channel_id=1, source_target_pairs={{0,16},{4,20},{8,24},{12,28},{16,0},{20,4},{24,8},{28,12},{1,17},{... | collective-permute-start | bytes 393224 | tf_op jit(solution)/shard_map/ppermute | solution.py:286
  4.8 24.4 %copy-start.1 = (bf16[256,256]{1,0:T(8,128)(2,1)S(1)}, bf16[256,256]{1,0:T(8,128)(2,1)}, u32[]{:S(2)}) copy-start(bf16[256,256]{1,0:T(8,128)(2,1)} %refs_4_.5) | copy-start | bytes 393220
  6.9 10.5 %collective-permute-start = (bf16[272,256]{1,0:T(8,128)(2,1)S(1)}, bf16[272,256]{1,0:T(8,128)(2,1)S(1)}, u32[]{:S(2)}, u32[]{:S(2)}) collective-permute-start(bf16[272,256]{1,0:T(8,128)(2,1)S(1)} %pad_maximum_fusion.refs_0_), channel_id=1, source_target_pairs={{0,16},{4,20},{8,24},{12,28},{16,0},{20,4},{24,8},{28,12},{1,17},{... | collective-permute-start | bytes 417800 | tf_op jit(solution)/shard_map/ppermute | solution.py:286
  7.1 11.9 %collective-permute-start.5 = (bf16[256,256]{1,0:T(8,128)(2,1)S(1)}, bf16[256,256]{1,0:T(8,128)(2,1)S(1)}, u32[]{:S(2)}, u32[]{:S(2)}) collective-permute-start(bf16[256,256]{1,0:T(8,128)(2,1)S(1)} %bitcast.5), channel_id=1, source_target_pairs={{0,8},{4,12},{8,0},{12,4},{16,24},{20,28},{24,16},{28,20},{1,9},{5... | collective-permute-start | bytes 393224 | tf_op jit(solution)/shard_map/ppermute | solution.py:286
  8.9 10.6 %collective-permute-start.4 = (bf16[256,256]{1,0:T(8,128)(2,1)S(1)}, bf16[256,256]{1,0:T(8,128)(2,1)S(1)}, u32[]{:S(2)}, u32[]{:S(2)}) collective-permute-start(bf16[256,256]{1,0:T(8,128)(2,1)S(1)} %bitcast.6), channel_id=1, source_target_pairs={{0,4},{4,0},{8,12},{12,8},{16,20},{20,16},{24,28},{28,24},{1,5},{5... | collective-permute-start | bytes 393224 | tf_op jit(solution)/shard_map/ppermute | solution.py:286
  14.9 6.2 %collective-permute-start.9 = (bf16[256,256]{1,0:T(8,128)(2,1)S(1)}, bf16[256,256]{1,0:T(8,128)(2,1)S(1)}, u32[]{:S(2)}, u32[]{:S(2)}) collective-permute-start(bf16[256,256]{1,0:T(8,128)(2,1)S(1)} %collective-permute-done.7.refs_6_), channel_id=1, source_target_pairs={{0,8},{4,12},{8,0},{12,4},{16,24},{20,28},{24,16},{28,20},{1,9},{5... | collective-permute-start | bytes 393224 | tf_op jit(solution)/shard_map/ppermute | solution.py:286
  15.2 8.1 %collective-permute-start.3 = (bf16[272,256]{1,0:T(8,128)(2,1)S(1)}, bf16[272,256]{1,0:T(8,128)(2,1)S(1)}, u32[]{:S(2)}, u32[]{:S(2)}) collective-permute-start(bf16[272,256]{1,0:T(8,128)(2,1)S(1)} %pad_maximum_fusion.refs_0_), channel_id=1, source_target_pairs={{0,4},{4,0},{8,12},{12,8},{16,20},{20,16},{24,28},{28,24},{1,5},{5... | collective-permute-start | bytes 417800 | tf_op jit(solution)/shard_map/ppermute | solution.py:286
  17.4 11.0 %collective-permute-start.1 = (bf16[272,256]{1,0:T(8,128)(2,1)S(1)}, bf16[272,256]{1,0:T(8,128)(2,1)S(1)}, u32[]{:S(2)}, u32[]{:S(2)}) collective-permute-start(bf16[272,256]{1,0:T(8,128)(2,1)S(1)} %collective-permute-done.refs_0_), channel_id=1, source_target_pairs={{0,8},{4,12},{8,0},{12,4},{16,24},{20,28},{24,16},{28,20},{1,9},{5... | collective-permute-start | bytes 417800 | tf_op jit(solution)/shard_map/ppermute | solution.py:286
  19.0 5.7 %collective-permute-start.8 = (bf16[256,256]{1,0:T(8,128)(2,1)S(1)}, bf16[256,256]{1,0:T(8,128)(2,1)S(1)}, u32[]{:S(2)}, u32[]{:S(2)}) collective-permute-start(bf16[256,256]{1,0:T(8,128)(2,1)S(1)} %collective-permute-done.7.refs_6_), channel_id=1, source_target_pairs={{0,4},{4,0},{8,12},{12,8},{16,20},{20,16},{24,28},{28,24},{1,5},{5... | collective-permute-start | bytes 393224 | tf_op jit(solution)/shard_map/ppermute | solution.py:286
  19.5 7.3 %collective-permute-start.6 = (bf16[256,256]{1,0:T(8,128)(2,1)S(1)}, bf16[256,256]{1,0:T(8,128)(2,1)S(1)}, u32[]{:S(2)}, u32[]{:S(2)}) collective-permute-start(bf16[256,256]{1,0:T(8,128)(2,1)S(1)} %collective-permute-done.4.refs_3_), channel_id=1, source_target_pairs={{0,8},{4,12},{8,0},{12,4},{16,24},{20,28},{24,16},{28,20},{1,9},{5... | collective-permute-start | bytes 393224 | tf_op jit(solution)/shard_map/ppermute | solution.py:286
  21.1 8.1 %collective-permute-start.10 = (bf16[256,256]{1,0:T(8,128)(2,1)S(1)}, bf16[256,256]{1,0:T(8,128)(2,1)S(1)}, u32[]{:S(2)}, u32[]{:S(2)}) collective-permute-start(bf16[256,256]{1,0:T(8,128)(2,1)S(1)} %collective-permute-done.9.refs_8_), channel_id=1, source_target_pairs={{0,4},{4,0},{8,12},{12,8},{16,20},{20,16},{24,28},{28,24},{1,5},{5... | collective-permute-start | bytes 393224 | tf_op jit(solution)/shard_map/ppermute | solution.py:286
  23.3 9.0 %collective-permute-start.12 = (bf16[272,256]{1,0:T(8,128)(2,1)S(1)}, bf16[272,256]{1,0:T(8,128)(2,1)S(1)}, u32[]{:S(2)}, u32[]{:S(2)}) collective-permute-start(bf16[272,256]{1,0:T(8,128)(2,1)S(1)} %pad_maximum_fusion.refs_0_), channel_id=1, source_target_pairs={{0,8},{4,12},{8,0},{12,4},{16,24},{20,28},{24,16},{28,20},{1,9},{5... | collective-permute-start | bytes 417800 | tf_op jit(solution)/shard_map/ppermute | solution.py:286
  24.7 10.9 %collective-permute-start.11 = (bf16[272,256]{1,0:T(8,128)(2,1)S(1)}, bf16[272,256]{1,0:T(8,128)(2,1)S(1)}, u32[]{:S(2)}, u32[]{:S(2)}) collective-permute-start(bf16[272,256]{1,0:T(8,128)(2,1)S(1)} %collective-permute-done.refs_0_), channel_id=1, source_target_pairs={{0,4},{4,0},{8,12},{12,8},{16,20},{20,16},{24,28},{28,24},{1,5},{5... | collective-permute-start | bytes 417800 | tf_op jit(solution)/shard_map/ppermute | solution.py:286
  26.9 5.5 %collective-permute-start.13 = (bf16[272,256]{1,0:T(8,128)(2,1)S(1)}, bf16[272,256]{1,0:T(8,128)(2,1)S(1)}, u32[]{:S(2)}, u32[]{:S(2)}) collective-permute-start(bf16[272,256]{1,0:T(8,128)(2,1)S(1)} %collective-permute-done.3.refs_1_), channel_id=1, source_target_pairs={{0,8},{4,12},{8,0},{12,4},{16,24},{20,28},{24,16},{28,20},{1,9},{5... | collective-permute-start | bytes 417800 | tf_op jit(solution)/shard_map/ppermute | solution.py:286
  28.3 10.5 %collective-permute-start.2 = (bf16[272,256]{1,0:T(8,128)(2,1)S(1)}, bf16[272,256]{1,0:T(8,128)(2,1)S(1)}, u32[]{:S(2)}, u32[]{:S(2)}) collective-permute-start(bf16[272,256]{1,0:T(8,128)(2,1)S(1)} %collective-permute-done.1.refs_0_), channel_id=1, source_target_pairs={{0,4},{4,0},{8,12},{12,8},{16,20},{20,16},{24,28},{28,24},{1,5},{5... | collective-permute-start | bytes 417800 | tf_op jit(solution)/shard_map/ppermute | solution.py:286
  42.3 1.6 %collective-permute-start.14 = (f32[256,256]{1,0:T(8,128)S(1)}, f32[256,256]{1,0:T(8,128)S(1)}, u32[]{:S(2)}, u32[]{:S(2)}) collective-permute-start(f32[256,256]{1,0:T(8,128)S(1)} %get-tuple-element.39), channel_id=1, source_target_pairs={{0,1},{1,0},{2,3},{3,2},{4,5},{5,4},{6,7},{7,6},{8,9},{9,8},{10,11... | collective-permute-start | bytes 786440 | tf_op jit(solution)/shard_map/ppermute | solution.py:282
  43.9 8.5 %collective-permute-start.15 = (f32[256,256]{1,0:T(8,128)S(1)}, f32[256,256]{1,0:T(8,128)S(1)}, u32[]{:S(2)}, u32[]{:S(2)}) collective-permute-start(f32[256,256]{1,0:T(8,128)S(1)} %add.11), channel_id=1, source_target_pairs={{0,2},{1,3},{2,0},{3,1},{4,6},{5,7},{6,4},{7,5},{8,10},{9,11},{10,... | collective-permute-start | bytes 786440 | tf_op jit(solution)/shard_map/ppermute | solution.py:282
  52.5 15.8 %collective-permute-start.16 = (f32[256,256]{1,0:T(8,128)S(1)}, f32[256,256]{1,0:T(8,128)S(1)}, u32[]{:S(2)}, u32[]{:S(2)}) collective-permute-start(f32[256,256]{1,0:T(8,128)S(1)} %add.12), channel_id=1, source_target_pairs={{0,1},{1,0},{2,3},{3,2},{4,5},{5,4},{6,7},{7,6},{8,9},{9,8},{10,11... | collective-permute-start | bytes 786440 | tf_op jit(solution)/shard_map/ppermute | solution.py:282
  54.5 7.6 %collective-permute-start.21 = (bf16[64,1024]{1,0:T(8,128)(2,1)S(1)}, bf16[64,1024]{1,0:T(8,128)(2,1)S(1)}, u32[]{:S(2)}, u32[]{:S(2)}) collective-permute-start(bf16[64,1024]{1,0:T(8,128)(2,1)S(1)} %get-tuple-element.46), channel_id=1, source_target_pairs={{0,1},{1,0},{2,3},{3,2},{4,5},{5,4},{6,7},{7,6},{8,9},{9,8},{10,11... | collective-permute-start | bytes 393224 | tf_op jit(solution)/shard_map/ppermute | solution.py:282
  57.4 8.4 %collective-permute-start.19 = (bf16[64,1024]{1,0:T(8,128)(2,1)S(1)}, bf16[64,1024]{1,0:T(8,128)(2,1)S(1)}, u32[]{:S(2)}, u32[]{:S(2)}) collective-permute-start(bf16[64,1024]{1,0:T(8,128)(2,1)S(1)} %get-tuple-element.44), channel_id=1, source_target_pairs={{0,2},{1,3},{2,0},{3,1},{4,6},{5,7},{6,4},{7,5},{8,10},{9,11},{10,... | collective-permute-start | bytes 393224 | tf_op jit(solution)/shard_map/ppermute | solution.py:282
  59.1 7.4 %collective-permute-start.17 = (bf16[64,1024]{1,0:T(8,128)(2,1)S(1)}, bf16[64,1024]{1,0:T(8,128)(2,1)S(1)}, u32[]{:S(2)}, u32[]{:S(2)}) collective-permute-start(bf16[64,1024]{1,0:T(8,128)(2,1)S(1)} %get-tuple-element.42), channel_id=1, source_target_pairs={{0,3},{1,2},{2,1},{3,0},{4,7},{5,6},{6,5},{7,4},{8,11},{9,10},{10,... | collective-permute-start | bytes 393224 | tf_op jit(solution)/shard_map/ppermute | solution.py:282
  59.2 1.2 %collective-permute-start.22 = (f32[1,1024]{1,0:T(1,128)S(1)}, f32[1,1024]{1,0:T(1,128)S(1)}, u32[]{:S(2)}, u32[]{:S(2)}) collective-permute-start(f32[1,1024]{1,0:T(1,128)S(1)} %get-tuple-element.43.refs_2_), channel_id=1, source_target_pairs={{0,1},{1,0},{2,3},{3,2},{4,5},{5,4},{6,7},{7,6},{8,9},{9,8},{10,11... | collective-permute-start | bytes 12296 | tf_op jit(solution)/shard_map/ppermute | solution.py:282
  60.4 5.4 %collective-permute-start.20 = (f32[1,1024]{1,0:T(1,128)S(1)}, f32[1,1024]{1,0:T(1,128)S(1)}, u32[]{:S(2)}, u32[]{:S(2)}) collective-permute-start(f32[1,1024]{1,0:T(1,128)S(1)} %get-tuple-element.43.refs_2_), channel_id=1, source_target_pairs={{0,2},{1,3},{2,0},{3,1},{4,6},{5,7},{6,4},{7,5},{8,10},{9,11},{10,... | collective-permute-start | bytes 12296 | tf_op jit(solution)/shard_map/ppermute | solution.py:282
  62.1 4.4 %collective-permute-start.18 = (f32[1,1024]{1,0:T(1,128)S(1)}, f32[1,1024]{1,0:T(1,128)S(1)}, u32[]{:S(2)}, u32[]{:S(2)}) collective-permute-start(f32[1,1024]{1,0:T(1,128)S(1)} %get-tuple-element.43.refs_2_), channel_id=1, source_target_pairs={{0,3},{1,2},{2,1},{3,0},{4,7},{5,6},{6,5},{7,4},{8,11},{9,10},{10,... | collective-permute-start | bytes 12296 | tf_op jit(solution)/shard_map/ppermute | solution.py:282
  (4 other events, 41.8 us)
